TPU v7x, 256 devices: a whole 4x4x8 slice. The times are simulated.
256 devices in a mesh: gx: 16 (over y_hi, z), gy: 16 (over x, y_lo, core).
Axes of the slice: x: 4, y: 4 (y_hi: 2, y_lo: 2; y = y_hi * 2 + y_lo), z: 8, core: 2. Of those that a mesh axis runs over, the one named last changes fastest.
Arguments:
- charge_density: float32 [256, 256, 256], P('gx', 'gy'), may hold values from -5080 to 5140
Outputs:
- potential: float32 [256, 256, 256], P('gx', 'gy')
- energies: float32 [2], replicated
All inputs are finite; a program needn't handle non-finite values.
Results may differ from a plain program's by a relative error of at most 0.0003.
Values sent between devices are 32-bit elements.
A program may use at most 128 MiB of HBM per device.

v0:
```python
import math

import jax
import jax.numpy as jnp
import numpy as np
from jax import lax
from jax.sharding import Mesh
from jax.sharding import PartitionSpec as P

ORDER = 16
GX = ("gx_0", "gx_1")
GY = ("gy_0", "gy_1", "gy_2")
GX_GY = ("gx_0", "gx_1", "gy_0", "gy_1", "gy_2")


exact_mode = lax.Precision.HIGHEST
outer_ratio = 1.1
radius_scale = math.sqrt(3.0) / 2.0


def over_axes(x, axes):
    for axis in axes:
        x = lax.psum(x, axis)
    return x


def sine_table(length):
    counter = jnp.arange(length, dtype=jnp.int32) + 1
    product = counter[:, None] * counter[None, :] % (2 * (length + 1))
    return jnp.sin(math.pi * product.astype(jnp.float32) / (length + 1))


def eigen_line(counter, length):
    half_angle = math.pi * (counter + 1).astype(jnp.float32) / (2.0 * (length + 1))
    return 4.0 * float((length + 1) * (length + 1)) * jnp.sin(half_angle) ** 2


def recurrence_tables():
    degree_count = ORDER + 1
    near_coeff = np.zeros((degree_count, degree_count, 1), np.float32)
    far_coeff = np.zeros((degree_count, degree_count, 1), np.float32)
    sector = np.ones(degree_count, np.float32)
    for degree in range(1, degree_count):
        for azimuth in range(degree):
            divisor = math.sqrt(degree * degree - azimuth * azimuth)
            near_coeff[degree, azimuth, 0] = (2 * degree - 1) / divisor
            far_coeff[degree, azimuth, 0] = (
                math.sqrt((degree - 1) * (degree - 1) - azimuth * azimuth) / divisor
            )
        if degree >= 2:
            sector[degree] = math.sqrt((2 * degree - 1) / (2.0 * degree))
    return (near_coeff, far_coeff, sector)


def expansion_weights():
    degree_count = ORDER + 1
    weights = np.zeros((degree_count, degree_count), np.float32)
    for degree in range(degree_count):
        for azimuth in range(degree + 1):
            factor = 1.0 if azimuth == 0 else 2.0
            weights[degree, azimuth] = factor / (
                4.0 * math.pi * radius_scale * outer_ratio ** (degree + 1)
            )
    return weights


def harmonic_sweep(unit_x, unit_y, unit_z, visitor, running):
    near_coeff, far_coeff, sector = recurrence_tables()
    degree_count = ORDER + 1
    selector = np.eye(degree_count, dtype=np.float32)[:, :, None]
    empty_rows = jnp.zeros((degree_count,) + unit_x.shape, unit_x.dtype)
    sector_cosine = jnp.ones_like(unit_x)
    sector_sine = jnp.zeros_like(unit_x)
    cosine_prev, sine_prev, cosine_old, sine_old = (empty_rows, empty_rows, empty_rows, empty_rows)
    for degree in range(degree_count):
        if degree > 0:
            sector_cosine, sector_sine = (
                sector[degree] * (unit_x * sector_cosine - unit_y * sector_sine),
                sector[degree] * (unit_x * sector_sine + unit_y * sector_cosine),
            )
        cosine_now = (
            near_coeff[degree] * unit_z * cosine_prev
            - far_coeff[degree] * cosine_old
            + selector[degree] * sector_cosine
        )
        sine_now = (
            near_coeff[degree] * unit_z * sine_prev
            - far_coeff[degree] * sine_old
            + selector[degree] * sector_sine
        )
        running = visitor(running, degree, cosine_now, sine_now)
        cosine_old, sine_old = (cosine_prev, sine_prev)
        cosine_prev, sine_prev = (cosine_now, sine_now)
    return running


def face_moments(point_x, point_y, point_z, charge):
    radius = jnp.sqrt(point_x * point_x + point_y * point_y + point_z * point_z)
    scaled_radius = radius / radius_scale

    def visitor(running, degree, cosine_now, sine_now):
        weight, moment_cosine, moment_sine, facing_cosine, facing_sine = running
        moment_cosine = moment_cosine + [jnp.dot(cosine_now, weight, precision=exact_mode)]
        moment_sine = moment_sine + [jnp.dot(sine_now, weight, precision=exact_mode)]
        facing_cosine = facing_cosine + [jnp.dot(cosine_now, charge, precision=exact_mode)]
        facing_sine = facing_sine + [jnp.dot(sine_now, charge, precision=exact_mode)]
        return (weight * scaled_radius, moment_cosine, moment_sine, facing_cosine, facing_sine)

    result = harmonic_sweep(
        point_x / radius, point_y / radius, point_z / radius, visitor, (charge, [], [], [], [])
    )
    return tuple((jnp.stack(listing) for listing in result[1:]))


def face_potential(point_x, point_y, point_z, weight_cosine, weight_sine):
    radius = jnp.sqrt(point_x * point_x + point_y * point_y + point_z * point_z)

    def visitor(accum, degree, cosine_now, sine_now):
        accum = accum + jnp.dot(weight_cosine[degree], cosine_now, precision=exact_mode)
        return accum + jnp.dot(weight_sine[degree], sine_now, precision=exact_mode)

    return harmonic_sweep(
        point_x / radius, point_y / radius, point_z / radius, visitor, jnp.zeros_like(point_x)
    )


def moments_of(points):
    return face_moments(points[0], points[1], points[2], points[3])


def no_moments(points):
    empty_rows = jnp.zeros((ORDER + 1, ORDER + 1), jnp.float32)
    return (empty_rows, empty_rows, empty_rows, empty_rows)


def potential_of(points):
    return face_potential(points[0], points[1], points[2], points[3], points[4])


def no_potential(points):
    return jnp.zeros_like(points[0])


def forward(volume, sine_rows, swap_one, swap_two):
    cells_a, cells_b, length = volume.shape
    spectrum = jnp.einsum("abz,zk->kab", volume, sine_rows, precision=exact_mode)
    spectrum = swap_one(spectrum.reshape(length, cells_a * cells_b))
    groups_one = spectrum.shape[1] // (cells_a * cells_b)
    pieces = spectrum.reshape(spectrum.shape[0], groups_one, cells_a, cells_b)
    table_one = sine_rows.reshape(groups_one, cells_a, length)
    spectrum = jnp.einsum("zpab,paj->jzb", pieces, table_one, precision=exact_mode)
    depth_cells = spectrum.shape[1]
    spectrum = swap_two(spectrum.reshape(length, depth_cells * cells_b))
    groups_two = spectrum.shape[1] // (depth_cells * cells_b)
    pieces = spectrum.reshape(spectrum.shape[0], groups_two, depth_cells, cells_b)
    table_two = sine_rows.reshape(groups_two, cells_b, length)
    return jnp.einsum("kqzc,qcj->kzj", pieces, table_two, precision=exact_mode)


def inverse(spectrum, sine_rows, back_two, back_one, cells_a, cells_b):
    rows_one, depth_cells, length = spectrum.shape
    groups_two = length // cells_b
    groups_one = length // cells_a
    table_two = sine_rows.reshape(length, groups_two, cells_b)
    pieces = jnp.einsum("kzj,jqc->kqzc", spectrum, table_two, precision=exact_mode)
    pieces = back_two(pieces.reshape(rows_one, groups_two * depth_cells * cells_b))
    pieces = pieces.reshape(length, depth_cells, cells_b)
    table_one = sine_rows.reshape(length, groups_one, cells_a)
    volume = jnp.einsum("jzb,jpa->zpab", pieces, table_one, precision=exact_mode)
    volume = back_one(volume.reshape(depth_cells, groups_one * cells_a * cells_b))
    volume = volume.reshape(length, cells_a, cells_b)
    return jnp.einsum("kab,kz->abz", volume, sine_rows, precision=exact_mode)


def shards(charge_density):
    cells_a, cells_b, length = charge_density.shape
    spacing = 1.0 / (length + 1)
    sine_rows = sine_table(length)
    index_x = lax.axis_index(GX)
    index_y = lax.axis_index(GY)

    def swap_one(operand):
        return lax.all_to_all(operand, GX, split_axis=0, concat_axis=1, tiled=True)

    def swap_two(operand):
        return lax.all_to_all(operand, GY, split_axis=0, concat_axis=1, tiled=True)

    def back_two(operand):
        return lax.all_to_all(operand, GY, split_axis=1, concat_axis=0, tiled=True)

    def back_one(operand):
        return lax.all_to_all(operand, GX, split_axis=1, concat_axis=0, tiled=True)

    groups_one = lax.axis_size(GX)
    groups_two = lax.axis_size(GY)
    count_one = length // groups_two
    count_two = length // groups_one
    eigen_one = eigen_line(index_y * count_one + jnp.arange(count_one, dtype=jnp.int32), length)
    eigen_two = eigen_line(index_x * count_two + jnp.arange(count_two, dtype=jnp.int32), length)
    eigen_full = eigen_line(jnp.arange(length, dtype=jnp.int32), length)
    denominator = (
        eigen_one[:, None, None] + eigen_two[None, :, None] + eigen_full[None, None, :]
    ) * ((length + 1) / 2.0) ** 3

    def back_of(spectrum):
        return inverse(spectrum, sine_rows, back_two, back_one, cells_a, cells_b)

    charge_spectrum = forward(charge_density, sine_rows, swap_one, swap_two) / denominator
    first_field = back_of(charge_spectrum)
    energy_first = spacing**3 * jnp.sum(charge_density * first_field)
    coords_x = (
        (index_x * cells_a + jnp.arange(cells_a, dtype=jnp.int32)).astype(jnp.float32)
        - (length - 1) / 2.0
    ) * spacing
    coords_y = (
        (index_y * cells_b + jnp.arange(cells_b, dtype=jnp.int32)).astype(jnp.float32)
        - (length - 1) / 2.0
    ) * spacing
    coords_z = (jnp.arange(length, dtype=jnp.float32) - (length - 1) / 2.0) * spacing
    face_x = jnp.broadcast_to(coords_x[:, None], (cells_a, cells_b)).reshape(-1)
    face_y = jnp.broadcast_to(coords_y[None, :], (cells_a, cells_b)).reshape(-1)
    plane_z = jnp.full((cells_a * cells_b,), 0.5, jnp.float32)
    side_y = jnp.broadcast_to(coords_y[:, None], (cells_b, length)).reshape(-1)
    side_depth_b = jnp.broadcast_to(coords_z[None, :], (cells_b, length)).reshape(-1)
    plane_b = jnp.full((cells_b * length,), 0.5, jnp.float32)
    side_x = jnp.broadcast_to(coords_x[:, None], (cells_a, length)).reshape(-1)
    side_depth_a = jnp.broadcast_to(coords_z[None, :], (cells_a, length)).reshape(-1)
    plane_a = jnp.full((cells_a * length,), 0.5, jnp.float32)
    boundary_faces = [
        (face_x, face_y, -plane_z, first_field[:, :, 0], None),
        (face_x, face_y, plane_z, first_field[:, :, -1], None),
        (-plane_b, side_y, side_depth_b, first_field[0], index_x == 0),
        (plane_b, side_y, side_depth_b, first_field[-1], index_x == lax.axis_size(GX) - 1),
        (side_x, -plane_a, side_depth_a, first_field[:, 0], index_y == 0),
        (side_x, plane_a, side_depth_a, first_field[:, -1], index_y == lax.axis_size(GY) - 1),
    ]
    totals = None
    for point_x, point_y, point_z, near_cells, owning in boundary_faces:
        points = (point_x, point_y, point_z, spacing * near_cells.reshape(-1))
        if owning is None:
            face_terms = moments_of(points)
        else:
            face_terms = lax.cond(owning, moments_of, no_moments, points)
        if totals is None:
            totals = face_terms
        else:
            totals = tuple((earlier + later for earlier, later in zip(totals, face_terms)))
    mom_cosine, mom_sine, dir_cosine, dir_sine = totals
    sum_cosine, sum_sine = (over_axes(mom_cosine, GX_GY), over_axes(mom_sine, GX_GY))
    weights = expansion_weights()
    weight_cosine = weights * sum_cosine
    weight_sine = weights * sum_sine
    potentials = []
    for point_x, point_y, point_z, near_cells, owning in boundary_faces:
        points = (point_x, point_y, point_z, weight_cosine, weight_sine)
        if owning is None:
            potentials.append(potential_of(points) / spacing**2)
        else:
            potentials.append(lax.cond(owning, potential_of, no_potential, points) / spacing**2)
    planes = jnp.stack(
        [potentials[0].reshape(cells_a, cells_b), potentials[1].reshape(cells_a, cells_b)]
    )
    planes = jnp.transpose(planes, (0, 2, 1))
    lead_walls = jnp.stack(
        [potentials[2].reshape(cells_b, length), potentials[3].reshape(cells_b, length)]
    )
    tail_walls = jnp.stack(
        [potentials[4].reshape(cells_a, length), potentials[5].reshape(cells_a, length)]
    )
    plane_width = 2 * cells_b * cells_a // count_two
    plane_part = jnp.broadcast_to(
        planes.reshape(1, count_two, plane_width), (groups_one, count_two, plane_width)
    ).reshape(length, plane_width)
    lead_depth = jnp.einsum("ftz,zk->kft", lead_walls, sine_rows, precision=exact_mode).reshape(
        length, 2 * cells_b
    )
    tail_depth = jnp.einsum("fbz,zk->kfb", tail_walls, sine_rows, precision=exact_mode).reshape(
        length, 2 * cells_a
    )
    received = swap_one(jnp.concatenate([plane_part, lead_depth, tail_depth], axis=1))
    received = received.reshape(count_two, groups_one, -1)
    plane_all = jnp.transpose(received[:, :, :plane_width], (1, 0, 2)).reshape(
        groups_one, 2, cells_b, cells_a
    )
    lead_total = jnp.sum(
        received[:, :, plane_width : plane_width + 2 * cells_b].reshape(
            count_two, groups_one, 2, cells_b
        ),
        axis=1,
    )
    tail_part = received[:, :, plane_width + 2 * cells_b :].reshape(
        count_two, groups_one, 2, cells_a
    )
    lead_table = sine_rows.reshape(groups_one, cells_a, length)
    plane_lead = jnp.einsum("pftb,pbj->jft", plane_all, lead_table, precision=exact_mode).reshape(
        length, 2 * cells_b
    )
    tail_lead = jnp.einsum("kpfb,pbj->jfk", tail_part, lead_table, precision=exact_mode).reshape(
        length, 2 * count_two
    )
    lead_width = 2 * count_two * cells_b // count_one
    lead_copies = jnp.broadcast_to(
        lead_total.reshape(1, count_one, lead_width), (groups_two, count_one, lead_width)
    ).reshape(length, lead_width)
    received = swap_two(jnp.concatenate([plane_lead, lead_copies, tail_lead], axis=1))
    received = received.reshape(count_one, groups_two, -1)
    tail_table = sine_rows.reshape(groups_two, cells_b, length)
    plane_modes = jnp.einsum(
        "jqft,qtm->jfm",
        received[:, :, : 2 * cells_b].reshape(count_one, groups_two, 2, cells_b),
        tail_table,
        precision=exact_mode,
    )
    lead_all = jnp.transpose(
        received[:, :, 2 * cells_b : 2 * cells_b + lead_width], (1, 0, 2)
    ).reshape(groups_two, count_two, 2, cells_b)
    lead_modes = jnp.einsum("qkft,qtm->fkm", lead_all, tail_table, precision=exact_mode)
    tail_modes = jnp.sum(
        received[:, :, 2 * cells_b + lead_width :].reshape(count_one, groups_two, 2, count_two),
        axis=1,
    )
    edge_rows = jnp.stack([sine_rows[0], sine_rows[-1]])
    depth_edge = lax.dynamic_slice_in_dim(edge_rows, index_x * count_two, count_two, 1)
    mode_edge = lax.dynamic_slice_in_dim(edge_rows, index_y * count_one, count_one, 1)
    result = jnp.einsum("jfm,fk->jkm", plane_modes, depth_edge, precision=exact_mode)
    result = result + jnp.einsum("fj,fkm->jkm", mode_edge, lead_modes, precision=exact_mode)
    potential = back_of(
        charge_spectrum
        + (result + jnp.einsum("jfk,fm->jkm", tail_modes, edge_rows, precision=exact_mode))
        / denominator
    )
    first_energy, second_energy = (
        over_axes(energy_first, GX_GY),
        over_axes(spacing**3 * jnp.sum(charge_density * potential), GX_GY),
    )
    return (potential, jnp.stack([first_energy, second_energy]))


def solution(mesh):
    torus = Mesh(mesh.devices.reshape(2, 8, 4, 2, 2), ("gx_0", "gx_1", "gy_0", "gy_1", "gy_2"))
    placed = (P(GX, GY, None),)
    return jax.shard_map(
        shards, mesh=torus, in_specs=placed, out_specs=(P(GX, GY, None), P()), check_vma=False
    )
```

profile of v0, /device:TPU:1, one launch (start us, length us, event | category | flops | bytes accessed | tf_op | source)
XLA Modules:
  0.0 501.1 jit_solution(20907520827085536)
XLA Ops:
  5.4 11.7 %all-to-all-start = ((f32[16,16,256]{2,1,0:T(8,128)}), f32[16,16,256]{2,1,0:T(8,128)S(1)}, u32[]{:S(2)}, u32[]{:S(2)}) async-start(f32[16,16,256]{2,1,0:T(8,128)} %copy.695), calls=%async_computation | async-start | bytes 524288 | tf_op jit(solution)/shard_map/all_to_all | solution.py:183
  17.5 10.0 %all-to-all-done = f32[16,16,256]{2,1,0:T(8,128)S(1)} async-done(((f32[16,16,256]{2,1,0:T(8,128)}), f32[16,16,256]{2,1,0:T(8,128)S(1)}, u32[]{:S(2)}, u32[]{:S(2)}) %all-to-all-start) | async-done | bytes 262176 | tf_op jit(solution)/shard_map/all_to_all | solution.py:183
  33.0 10.4 %fusion.1217 = f32[16,16,256]{2,1,0:T(8,128)} fusion(f32[256,16,16,1]{0,2,1,3:T(8,128)S(1)} %reshape.1732, s32[16,16]{1,0:T(8,128)S(1)} %get-tuple-element.3307, s32[16,16]{1,0:T(8,128)S(1)} %get-tuple-element.3306), kind=kOutput, calls=%fused_computation.1802 | convolution fusion | flops 201916416 | bytes 526336 | tf_op jit(solution)/shard_map/zpab,paj->jzb/dot_general | solution.py:151
  91.2 9.9 %all-to-all-done.3 = f32[16,16,256]{2,0,1:T(8,128)S(1)} async-done(((f32[16,16,256]{2,0,1:T(8,128)}), f32[16,16,256]{2,0,1:T(8,128)S(1)}, u32[]{:S(2)}, u32[]{:S(2)}) %all-to-all-start.3) | async-done | bytes 262176 | tf_op jit(solution)/shard_map/all_to_all | solution.py:192
  125.2 8.8 %conditional.9 = (f32[17,17]{1,0:T(8,128)S(1)}, f32[17,17]{1,0:T(8,128)S(1)}) conditional(s32[]{:T(128)} %convert_element_type.116, () %tuple.66, (f32[17,1]{0,1:T(1,128)S(1)}, f32[4096]{0:T(1024)S(1)}, f32[4096]{0:T(1024)S(1)}, f32[4096]{0:T(1024)S(1)}, f32[17,1]{0,1:T(1,128)S(1)}, /*index=5*/f32[17,1]{0,1:T(1,128)S(1)}, ...), branch_computations={%region_2.3_spmd, %region_3.4_spmd} | conditional | flops 72704088 | bytes 13647684 | solution.py:243
  134.1 27.5 %conditional.8 = (f32[17,17]{1,0:T(8,128)S(1)}, f32[17,17]{1,0:T(8,128)S(1)}) conditional(s32[]{:T(128)} %convert_element_type.115, () %tuple.64, (f32[17,1]{0,1:T(1,128)S(1)}, f32[4096]{0:T(1024)S(1)}, f32[4096]{0:T(1024)S(1)}, f32[4096]{0:T(1024)S(1)}, f32[17,1]{0,1:T(1,128)S(1)}, /*index=5*/f32[17,1]{0,1:T(1,128)S(1)}, ...), branch_computations={%region_0.1_spmd, %region_1.2_spmd} | conditional | flops 72704088 | bytes 13647684 | solution.py:243
  161.6 14.8 %conditional.11 = (f32[17,17]{1,0:T(8,128)S(1)}, f32[17,17]{1,0:T(8,128)S(1)}) conditional(s32[]{:T(128)} %convert_element_type.118, () %tuple.69, (f32[17,1]{0,1:T(1,128)S(1)}, f32[4096]{0:T(1024)S(1)}, f32[4096]{0:T(1024)S(1)}, f32[4096]{0:T(1024)S(1)}, f32[17,1]{0,1:T(1,128)S(1)}, /*index=5*/f32[17,1]{0,1:T(1,128)S(1)}, ...), branch_computations={%region_6.7_spmd, %region_7.8_spmd} | conditional | flops 72704088 | bytes 13614916 | solution.py:243
  176.5 10.8 %conditional.10 = (f32[17,17]{1,0:T(8,128)S(1)}, f32[17,17]{1,0:T(8,128)S(1)}) conditional(s32[]{:T(128)} %convert_element_type.117, () %tuple.67, (f32[17,1]{0,1:T(1,128)S(1)}, f32[4096]{0:T(1024)S(1)}, f32[4096]{0:T(1024)S(1)}, f32[4096]{0:T(1024)S(1)}, f32[17,1]{0,1:T(1,128)S(1)}, /*index=5*/f32[17,1]{0,1:T(1,128)S(1)}, ...), branch_computations={%region_4.5_spmd, %region_5.6_spmd} | conditional | flops 72704088 | bytes 13614916 | solution.py:243
  194.1 29.4 %all-reduce.1 = (f32[17,17]{1,0:T(8,128)S(1)}, f32[17,17]{1,0:T(8,128)S(1)}) all-reduce(f32[17,17]{1,0:T(8,128)S(1)} %get-tuple-element.2624, f32[17,17]{1,0:T(8,128)S(1)} %get-tuple-element.2625), channel_id=1, replica_groups=mesh['gx_0'=2,'gx_1'=8,'gy_0'=4,'gy_1'=2,'gy_2'=2] {'gx_1'}, use_global_device_ids=true, to_apply=%region_9.10 | all-reduce | flops 578 | bytes 4624 | tf_op jit(solution)/shard_map/psum | solution.py:23
  223.5 11.3 %all-reduce.3 = (f32[17,17]{1,0:T(8,128)S(1)}, f32[17,17]{1,0:T(8,128)S(1)}) all-reduce(f32[17,17]{1,0:T(8,128)S(1)} %get-tuple-element.2608, f32[17,17]{1,0:T(8,128)S(1)} %get-tuple-element.2609), channel_id=1, replica_groups=mesh['gx_0'=2,'gx_1'=8,'gy_0'=4,'gy_1'=2,'gy_2'=2] {'gy_0'}, use_global_device_ids=true, to_apply=%region_10.11 | all-reduce | flops 578 | bytes 4624 | tf_op jit(solution)/shard_map/psum | solution.py:23
  234.7 18.0 %all-reduce.7 = (f32[17,17]{1,0:T(8,128)S(1)}, f32[17,17]{1,0:T(8,128)S(1)}) all-reduce(f32[17,17]{1,0:T(8,128)S(1)} %get-tuple-element.2612, f32[17,17]{1,0:T(8,128)S(1)} %get-tuple-element.2613), channel_id=1, replica_groups=mesh['gx_0'=2,'gx_1'=8,'gy_0'=4,'gy_1'=2,'gy_2'=2] {'gy_1'}, use_global_device_ids=true, to_apply=%region_11.12 | all-reduce | flops 578 | bytes 4624 | tf_op jit(solution)/shard_map/psum | solution.py:23
  252.7 23.4 %all-reduce.5 = (f32[17,17]{1,0:T(8,128)S(1)}, f32[17,17]{1,0:T(8,128)S(1)}) all-reduce(f32[17,17]{1,0:T(8,128)S(1)} %get-tuple-element.2620, f32[17,17]{1,0:T(8,128)S(1)} %get-tuple-element.2621), channel_id=1, replica_groups=mesh['gx_0'=2,'gx_1'=8,'gy_0'=4,'gy_1'=2,'gy_2'=2] {'gy_2'}, use_global_device_ids=true, to_apply=%region_12.13 | all-reduce | flops 578 | bytes 4624 | tf_op jit(solution)/shard_map/psum | solution.py:23
  288.5 8.6 %conditional.13 = (f32[4096]{0:T(1024)S(1)}) conditional(s32[]{:T(128)} %convert_element_type.116, () %tuple.72, (f32[17,1]{0,1:T(1,128)S(1)}, f32[4096]{0:T(1024)S(1)}, f32[4096]{0:T(1024)S(1)}, f32[4096]{0:T(1024)S(1)}, f32[17,1]{0,1:T(1,128)S(1)}, /*index=5*/f32[17,1]{0,1:T(1,128)S(1)}, f32[17,17]{1,0:T(8,128)S(1)}, f32[17,1]{0,1:T(1,128)S(1)}, ...), branch_computations={%region_20.21_spmd, %region_21.22_spmd} | conditional | flops 72646736 | bytes 16684288 | solution.py:259
  297.1 24.6 %conditional.12 = (f32[4096]{0:T(1024)S(1)}) conditional(s32[]{:T(128)} %convert_element_type.115, () %tuple.70, (f32[17,1]{0,1:T(1,128)S(1)}, f32[4096]{0:T(1024)S(1)}, f32[4096]{0:T(1024)S(1)}, f32[4096]{0:T(1024)S(1)}, f32[17,1]{0,1:T(1,128)S(1)}, /*index=5*/f32[17,1]{0,1:T(1,128)S(1)}, f32[17,17]{1,0:T(8,128)S(1)}, f32[17,1]{0,1:T(1,128)S(1)}, ...), branch_computations={%region_18.19_spmd, %region_19.20_spmd} | conditional | flops 72646736 | bytes 16684288 | solution.py:259
  321.8 14.9 %conditional.15 = (f32[4096]{0:T(1024)S(1)}) conditional(s32[]{:T(128)} %convert_element_type.118, () %tuple.75, (f32[17,1]{0,1:T(1,128)S(1)}, f32[4096]{0:T(1024)S(1)}, f32[4096]{0:T(1024)S(1)}, f32[4096]{0:T(1024)S(1)}, f32[17,1]{0,1:T(1,128)S(1)}, /*index=5*/f32[17,1]{0,1:T(1,128)S(1)}, f32[17,17]{1,0:T(8,128)S(1)}, f32[17,1]{0,1:T(1,128)S(1)}, ...), branch_computations={%region_24.25_spmd, %region_25.26_spmd} | conditional | flops 72646736 | bytes 16684288 | solution.py:259
  336.6 9.1 %conditional.14 = (f32[4096]{0:T(1024)S(1)}) conditional(s32[]{:T(128)} %convert_element_type.117, () %tuple.73, (f32[17,1]{0,1:T(1,128)S(1)}, f32[4096]{0:T(1024)S(1)}, f32[4096]{0:T(1024)S(1)}, f32[4096]{0:T(1024)S(1)}, f32[17,1]{0,1:T(1,128)S(1)}, /*index=5*/f32[17,1]{0,1:T(1,128)S(1)}, f32[17,17]{1,0:T(8,128)S(1)}, f32[17,1]{0,1:T(1,128)S(1)}, ...), branch_computations={%region_22.23_spmd, %region_23.24_spmd} | conditional | flops 72646736 | bytes 16684288 | solution.py:259
  357.9 7.6 %all-to-all-done.4 = f32[16,16,96]{2,1,0:T(8,128)S(1)} async-done(((f32[16,16,96]{2,1,0:T(8,128)}), f32[16,16,96]{2,1,0:T(8,128)S(1)}, u32[]{:S(2)}, u32[]{:S(2)}) %all-to-all-start.4) | async-done | bytes 98336 | tf_op jit(solution)/shard_map/all_to_all | solution.py:183
  365.9 9.7 %fusion.1222 = f32[16,16,32]{2,1,0:T(8,128)S(1)} fusion(s32[16,16]{1,0:T(8,128)S(1)} %copy-done.4, s32[16,16]{1,0:T(8,128)S(1)} %copy-done.75, f32[32,16,16]{0,2,1:T(8,128)S(1)} %copy.699), kind=kOutput, calls=%fused_computation.1806 | convolution fusion | flops 25755648 | bytes 67584 | tf_op jit(solution)/shard_map/pftb,pbj->jft/dot_general | solution.py:295
  378.9 20.3 %all-to-all-start.5 = ((f32[16,16,96]{2,1,0:T(8,128)}), f32[16,16,96]{2,1,0:T(8,128)S(1)}, u32[]{:S(2)}, u32[]{:S(2)}) async-start(f32[16,16,96]{2,1,0:T(8,128)} %pad_maximum_fusion.1), calls=%async_computation.5 | async-start | bytes 262144 | tf_op jit(solution)/shard_map/all_to_all | solution.py:186
  417.7 10.5 %all_to_all.119 = f32[16,16,256]{2,0,1:T(8,128)S(1)} all-to-all(f32[16,16,256]{2,0,1:T(8,128)S(1)} %reshape.2029), channel_id=1, replica_groups=mesh['gx_0'=2,'gx_1'=8,'gy_0'=4,'gy_1'=2,'gy_2'=2] {'gy_0','gy_1','gy_2'}, dimensions={1} | all-to-all | bytes 524288 | tf_op jit(solution)/shard_map/all_to_all | solution.py:189
  433.6 13.2 %all_to_all.120 = f32[16,16,256]{2,0,1:T(8,128)S(1)} all-to-all(f32[16,16,256]{2,0,1:T(8,128)S(1)} %all_to_all.108), channel_id=1, replica_groups=mesh['gx_0'=2,'gx_1'=8,'gy_0'=4,'gy_1'=2,'gy_2'=2] {'gx_0','gx_1'}, dimensions={1} | all-to-all | bytes 524288 | tf_op jit(solution)/shard_map/all_to_all | solution.py:192
  460.6 13.6 %all-reduce = (f32[]{:T(128)}, f32[]{:T(128)}) all-reduce(f32[]{:T(128)} %get-tuple-element.2622, f32[]{:T(128)} %get-tuple-element.2623), channel_id=1, replica_groups=mesh['gx_0'=2,'gx_1'=8,'gy_0'=4,'gy_1'=2,'gy_2'=2] {'gx_1'}, use_global_device_ids=true, to_apply=%region_36.37 | all-reduce | flops 2 | bytes 16 | tf_op jit(solution)/shard_map/psum | solution.py:23
  474.2 7.9 %all-reduce.2 = (f32[]{:T(128)}, f32[]{:T(128)}) all-reduce(f32[]{:T(128)} %get-tuple-element.2606, f32[]{:T(128)} %get-tuple-element.2607), channel_id=1, replica_groups=mesh['gx_0'=2,'gx_1'=8,'gy_0'=4,'gy_1'=2,'gy_2'=2] {'gy_0'}, use_global_device_ids=true, to_apply=%region_37.38 | all-reduce | flops 2 | bytes 16 | tf_op jit(solution)/shard_map/psum | solution.py:23
  486.7 12.4 %all-reduce.4 = (f32[1]{0:T(128)}, f32[1]{0:T(128)}) all-reduce(f32[1]{0:T(128)} %bitcast.1850, f32[1]{0:T(128)} %bitcast.1849), channel_id=1, replica_groups=mesh['gx_0'=2,'gx_1'=8,'gy_0'=4,'gy_1'=2,'gy_2'=2] {'gy_2'}, use_global_device_ids=true, to_apply=%region_39.40 | all-reduce | flops 2 | bytes 16 | tf_op jit(solution)/shard_map/psum | solution.py:23
  (529 shorter events, 210.1 us)
Async XLA Ops:
  0.6 101.2 %copy-start.50 = (s32[256]{0:T(256)}, s32[256]{0:T(256)S(1)}, u32[]{:S(2)}) copy-start(s32[256]{0:T(256)S(1)} %iota_add_fusion) | copy-start | bytes 3076
  5.4 22.0 %all-to-all-start = ((f32[16,16,256]{2,1,0:T(8,128)}), f32[16,16,256]{2,1,0:T(8,128)S(1)}, u32[]{:S(2)}, u32[]{:S(2)}) async-start(f32[16,16,256]{2,1,0:T(8,128)} %copy.695), calls=%async_computation | async-start | bytes 524288 | tf_op jit(solution)/shard_map/all_to_all | solution.py:183
  17.2 41.1 %copy-start.76 = (f32[256]{0:T(256)}, f32[256]{0:T(256)S(1)}, u32[]{:S(2)}) copy-start(f32[256]{0:T(256)S(1)} %multiply_multiply_fusion.64) | copy-start | bytes 3076
  17.2 15.8 %copy-start.74 = (s32[16,16]{1,0:T(8,128)}, s32[16,16]{1,0:T(8,128)S(1)}, u32[]{:S(2)}) copy-start(s32[16,16]{1,0:T(8,128)S(1)} %get-tuple-element.3306) | copy-start | bytes 3076
  17.2 64.1 %copy-start.3 = (s32[16,16]{1,0:T(8,128)}, s32[16,16]{1,0:T(8,128)S(1)}, u32[]{:S(2)}) copy-start(s32[16,16]{1,0:T(8,128)S(1)} %get-tuple-element.3307) | copy-start | bytes 3076
  17.4 40.9 %copy-start.52 = (f32[16,16]{1,0:T(8,128)}, f32[16,16]{1,0:T(8,128)S(1)}, u32[]{:S(2)}) copy-start(f32[16,16]{1,0:T(8,128)S(1)} %broadcast_add_fusion) | copy-start | bytes 3076
  43.4 14.3 %all-to-all-start.1 = ((f32[16,16,256]{2,1,0:T(8,128)}), f32[16,16,256]{2,1,0:T(8,128)S(1)}, u32[]{:S(2)}, u32[]{:S(2)}) async-start(f32[16,16,256]{2,1,0:T(8,128)} %fusion.1217), calls=%async_computation.1 | async-start | bytes 524288 | tf_op jit(solution)/shard_map/all_to_all | solution.py:186
  68.5 11.2 %all-to-all-start.2 = ((f32[16,16,256]{2,0,1:T(8,128)}), f32[16,16,256]{2,0,1:T(8,128)S(1)}, u32[]{:S(2)}, u32[]{:S(2)}) async-start(f32[16,16,256]{2,0,1:T(8,128)} %reshape.2024), calls=%async_computation.2 | async-start | bytes 524288 | tf_op jit(solution)/shard_map/all_to_all | solution.py:189
  85.7 15.4 %all-to-all-start.3 = ((f32[16,16,256]{2,0,1:T(8,128)}), f32[16,16,256]{2,0,1:T(8,128)S(1)}, u32[]{:S(2)}, u32[]{:S(2)}) async-start(f32[16,16,256]{2,0,1:T(8,128)} %all_to_all.98), calls=%async_computation.3 | async-start | bytes 524288 | tf_op jit(solution)/shard_map/all_to_all | solution.py:192
  111.7 13.1 %copy-start.2 = (f32[17,1]{0,1:T(1,128)S(1)}, f32[17,1]{0,1:T(1,128)}, u32[]{:S(2)}) copy-start(f32[17,1]{0,1:T(1,128)} %constant.561.clone) | copy-start | bytes 208
  111.7 13.1 %copy-start.6 = (f32[17,1]{0,1:T(1,128)S(1)}, f32[17,1]{0,1:T(1,128)}, u32[]{:S(2)}) copy-start(f32[17,1]{0,1:T(1,128)} %constant.598.clone) | copy-start | bytes 208
  111.7 13.1 %copy-start.7 = (f32[17,1]{0,1:T(1,128)S(1)}, f32[17,1]{0,1:T(1,128)}, u32[]{:S(2)}) copy-start(f32[17,1]{0,1:T(1,128)} %constant.597.clone) | copy-start | bytes 208
  111.7 13.1 %copy-start.8 = (f32[17,1]{0,1:T(1,128)S(1)}, f32[17,1]{0,1:T(1,128)}, u32[]{:S(2)}) copy-start(f32[17,1]{0,1:T(1,128)} %constant.596.clone) | copy-start | bytes 208
  111.7 13.1 %copy-start.9 = (f32[17,1]{0,1:T(1,128)S(1)}, f32[17,1]{0,1:T(1,128)}, u32[]{:S(2)}) copy-start(f32[17,1]{0,1:T(1,128)} %constant.595.clone) | copy-start | bytes 208
  111.7 13.1 %copy-start.10 = (f32[17,1]{0,1:T(1,128)S(1)}, f32[17,1]{0,1:T(1,128)}, u32[]{:S(2)}) copy-start(f32[17,1]{0,1:T(1,128)} %constant.594.clone) | copy-start | bytes 208
  176.5 99.7 %copy-start.56 = (f32[17,17]{1,0:T(8,128)S(1)}, f32[17,17]{1,0:T(8,128)}, u32[]{:S(2)}) copy-start(f32[17,17]{1,0:T(8,128)} %constant.608.clone) | copy-start | bytes 3472
  347.5 18.4 %copy-start.4 = (s32[16,16]{1,0:T(8,128)S(1)}, s32[16,16]{1,0:T(8,128)}, u32[]{:S(2)}) copy-start(s32[16,16]{1,0:T(8,128)} %copy-done.3) | copy-start | bytes 3076
  347.5 18.4 %copy-start.75 = (s32[16,16]{1,0:T(8,128)S(1)}, s32[16,16]{1,0:T(8,128)}, u32[]{:S(2)}) copy-start(s32[16,16]{1,0:T(8,128)} %copy-done.74) | copy-start | bytes 3076
  349.9 15.6 %all-to-all-start.4 = ((f32[16,16,96]{2,1,0:T(8,128)}), f32[16,16,96]{2,1,0:T(8,128)S(1)}, u32[]{:S(2)}, u32[]{:S(2)}) async-start(f32[16,16,96]{2,1,0:T(8,128)} %pad_maximum_fusion), calls=%async_computation.4 | async-start | bytes 262144 | tf_op jit(solution)/shard_map/all_to_all | solution.py:183
  378.9 31.3 %copy-start.1 = (f32[16,16,256]{2,1,0:T(8,128)S(1)}, f32[16,16,256]{2,1,0:T(8,128)}, u32[]{:S(2)}) copy-start(f32[16,16,256]{2,1,0:T(8,128)} %copy-done) | copy-start | bytes 786436
  378.9 31.3 %copy-start.53 = (f32[16,16]{1,0:T(8,128)S(1)}, f32[16,16]{1,0:T(8,128)}, u32[]{:S(2)}) copy-start(f32[16,16]{1,0:T(8,128)} %copy-done.52) | copy-start | bytes 3076
  378.9 31.3 %copy-start.77 = (f32[256]{0:T(256)S(1)}, f32[256]{0:T(256)}, u32[]{:S(2)}) copy-start(f32[256]{0:T(256)} %copy-done.76) | copy-start | bytes 3076
  378.9 26.5 %all-to-all-start.5 = ((f32[16,16,96]{2,1,0:T(8,128)}), f32[16,16,96]{2,1,0:T(8,128)S(1)}, u32[]{:S(2)}, u32[]{:S(2)}) async-start(f32[16,16,96]{2,1,0:T(8,128)} %pad_maximum_fusion.1), calls=%async_computation.5 | async-start | bytes 262144 | tf_op jit(solution)/shard_map/all_to_all | solution.py:186
  432.7 14.8 %copy-start.5 = (f32[16,16,256]{2,1,0:T(8,128)S(1)}, f32[16,16,256]{2,1,0:T(8,128)}, u32[]{:S(2)}) copy-start(f32[16,16,256]{2,1,0:T(8,128)} %param.630) | copy-start | bytes 786436
  (69 other events, 614.1 us)
where the time goes:
time: 507 us; the launch traced here: 501 us
  blocking collectives  157 us (31%)
  matrix products  124 us (24%)
  loops' own time  68 us (13%)
  starting transfers between devices  54.7 us (11%)
  waiting for transfers between devices  47.2 us (9%)
  local copies, waits for them, and re-layouts  27.8 us (5%)
  other arithmetic  18.8 us (4%)
    psum x10, blocking collectives, over_axes(): x = lax.psum(x, axis)  133 us
    another operation x4, loops' own time, shards(): face_terms = lax.cond(owning, moments_of, no_moments, points)  35 us
    another operation x4, loops' own time, shards(): lax.cond(owning, potential_of, no_potential, points) / spacing ** 2  33 us
    all_to_all x2, starting transfers between devices, swap_two(): return lax.all_to_all(operand, GY, split_axis=0, concat_axis=1, tiled=True)  27.3 us
    all_to_all x2, starting transfers between devices, swap_one(): return lax.all_to_all(operand, GX, split_axis=0, concat_axis=1, tiled=True)  18.6 us
    dot_general x51, matrix products, visitor(): jnp.dot(cosine_now, weight, precision=exact_mode)  17.7 us
    all_to_all x2, waiting for transfers between devices, swap_one(): return lax.all_to_all(operand, GX, split_axis=0, concat_axis=1, tiled=True)  17.6 us
    dot_general x51, matrix products, visitor(): jnp.dot(sine_now, weight, precision=exact_mode)  17.6 us
  transfers between devices with their start and end apart: 6, of which 6 were waited for; matrix products, arithmetic and copies ran while one was open for 1% of the time, Pallas kernels for 0%

commit v1 on v0

v1 whole, which is shorter than its diff:
```python
import math

import jax
import jax.numpy as jnp
import numpy as np
from jax import lax
from jax.sharding import PartitionSpec as P

ORDER = 16
N = 256
SLOTS = 48
LANES = 1024
SPARE = 7 * 128 + 112
ENERGY_LANE = 1023


def harmonics(x, y, z):
    cosine = {(0, 0): np.ones_like(x)}
    sine = {(0, 0): np.zeros_like(x)}
    for l in range(1, ORDER + 1):
        scale = 1.0 if l == 1 else math.sqrt((2 * l - 1) / (2.0 * l))
        c, s = cosine[l - 1, l - 1], sine[l - 1, l - 1]
        cosine[l, l] = scale * (x * c - y * s)
        sine[l, l] = scale * (x * s + y * c)
        for m in range(l):
            near = (2 * l - 1) / math.sqrt(l * l - m * m)
            far = math.sqrt((l - 1) ** 2 - m * m) / math.sqrt(l * l - m * m)
            for table in (cosine, sine):
                older = table[l - 2, m] if l - 2 >= m else 0.0
                table[l, m] = near * z * table[l - 1, m] - far * older
    return cosine, sine


def face_point(face, t, s):
    one = np.ones_like(t)
    return ((t, s, one), (one, s, t), (t, one, s))[face]


def face_parity(face, px, py, pz):
    return ((px, py, pz), (pz, py, px), (px, pz, py))[face]


def trig(parity, odd, angle):
    if odd:
        orders = np.arange(1, 16, 2)
    else:
        orders = np.arange(0, 17, 2) if parity == 0 else np.arange(2, 17, 2)
    wave = np.cos if parity == 0 else np.sin
    return wave(orders[:, None] * angle[None, :])


def build_tables():
    span = N + 1.0
    step = 1.0 / span
    radius = math.sqrt(3.0) / 2.0
    index = np.arange(N) + 1
    sine_rows = np.sin(np.pi * (index[:, None] * index[None, :] % (2 * N + 2)) / span)
    eigen = 4.0 * span * span * np.sin(np.pi * index / (2 * span)) ** 2
    scaled = 2.0 * (np.arange(N) - (N - 1) / 2.0) * step
    angle = np.arctan(scaled)

    terms = [[] for _ in range(8)]
    for l in range(ORDER + 1):
        for m in range(l + 1):
            terms[(m % 2) * 4 + (l - m) % 2].append((l, m, 0))
            if m:
                terms[((m - 1) % 2) * 4 + 2 + (l - m) % 2].append((l, m, 1))

    nodes, quad = np.polynomial.legendre.leggauss(24)
    legendre = np.polynomial.legendre.legvander(nodes, ORDER).T
    basis = np.zeros((N, 32))
    basis[:, : ORDER + 1] = sine_rows @ np.polynomial.legendre.legvander(scaled, ORDER)
    even = (np.arange(N) % 2 == 0).astype(np.float64)
    basis[:, 17] = sine_rows[0] * even
    basis[:, 18] = sine_rows[0] * (1.0 - even)
    project = legendre * quad[None, :] * (np.arange(ORDER + 1) + 0.5)[:, None]
    turns = 64
    circle = 2.0 * np.pi * np.arange(turns) / turns
    ones_t, ones_s = np.meshgrid(nodes, nodes, indexing="ij")
    alpha, beta = np.meshgrid(circle, circle, indexing="ij")
    solid, wave = [], []
    for face in range(3):
        x, y, z = face_point(face, ones_t, ones_s)
        r = np.sqrt(x * x + y * y + z * z)
        table = harmonics(x / r, y / r, z / r)
        solid.append((table, r / math.sqrt(3.0)))
        ca, sa, cb, sb = np.cos(alpha), np.sin(alpha), np.cos(beta), np.sin(beta)
        parts = (sa * cb, ca * sb, ca * cb)
        x, y, z = (parts, (parts[2], parts[1], parts[0]), (parts[0], parts[2], parts[1]))[face]
        r = np.sqrt(x * x + y * y + z * z)
        safe = np.where(r < 1e-12, 1.0, r)
        wave.append((harmonics(x / safe, y / safe, z / safe), np.where(r < 1e-12, 0.0, r)))

    select = np.zeros((3, 32, LANES))
    gather = np.zeros((SLOTS, LANES))
    spread = np.zeros((SLOTS, 16, 256))
    columns = np.zeros((256, N))
    rows = np.zeros((8, 3, 16, N))
    spill = SPARE
    for group in range(8):
        px, py, pz = group >> 2 & 1, group >> 1 & 1, group & 1
        odd = (px + py + pz) % 2
        lane = group * 128
        for face in range(3):
            prow, pcol, normal = face_parity(face, px, py, pz)
            sign = 2.0 if normal == 0 else -2.0
            entries = [
                (i, j)
                for i in range(prow, ORDER + 1, 2)
                for j in range(pcol, ORDER + 1, 2)
                if i + j + normal <= ORDER - odd
            ]
            moments = {}
            for slot, (l, m, which) in enumerate(terms[group]):
                table, ratio = solid[face]
                values = ratio**l * table[which][l, m]
                moments[slot] = project @ values @ project.T
            for i, j in entries:
                if lane >= (group + 1) * 128 or (lane >= SPARE and group == 7):
                    position, spill = spill, spill + 1
                    assert group == 0
                else:
                    position, lane = lane, lane + 1
                axes = ((0, 1, 2), (2, 1, 0), (0, 2, 1))[face]
                select[axes[0], i, position] = 1.0
                select[axes[1], j, position] = 1.0
                select[axes[2], 17 + normal, position] = 1.0
                for slot in moments:
                    gather[slot, position] = step * sign * moments[slot][i, j]
            left = trig(prow, odd, circle)
            right = trig(pcol, odd, circle)
            left_unit = left / np.sum(left * left, axis=1, keepdims=True)
            right_unit = right / np.sum(right * right, axis=1, keepdims=True)
            base = group * 32 + face * 9
            for slot, (l, m, which) in enumerate(terms[group]):
                table, r = wave[face]
                values = r ** (ORDER - odd) * table[which][l, m]
                block = left_unit @ values @ right_unit.T
                weight = (1.0 if m == 0 else 2.0) / (4.0 * math.pi * radius * 1.1 ** (l + 1))
                block = block * weight * sign * span * span
                spread[slot, : block.shape[0], base : base + block.shape[1]] = block
            tail = trig(pcol, odd, angle)
            columns[base : base + tail.shape[0]] = tail
            head = trig(prow, odd, angle)
            rows[group, face, : head.shape[0]] = head
    assert spill < ENERGY_LANE
    root = 1.0 / np.sqrt(1.0 - np.outer(np.sin(angle) ** 2, np.sin(angle) ** 2))
    return sine_rows, eigen, basis, select, gather, spread, columns, rows, root, root**15


mode = lax.Precision.HIGH


def transform_forward(volume, sine_rows, swap_one, swap_two):
    cells_a, cells_b, length = volume.shape
    spectrum = jnp.einsum("abz,zk->kab", volume, sine_rows, precision=mode)
    spectrum = swap_one(spectrum.reshape(length, cells_a * cells_b))
    groups = spectrum.shape[1] // (cells_a * cells_b)
    pieces = spectrum.reshape(spectrum.shape[0], groups, cells_a, cells_b)
    table = sine_rows.reshape(groups, cells_a, length)
    spectrum = jnp.einsum("zpab,paj->jzb", pieces, table, precision=mode)
    depth = spectrum.shape[1]
    spectrum = swap_two(spectrum.reshape(length, depth * cells_b))
    groups = spectrum.shape[1] // (depth * cells_b)
    pieces = spectrum.reshape(spectrum.shape[0], groups, depth, cells_b)
    table = sine_rows.reshape(groups, cells_b, length)
    return jnp.einsum("kqzc,qcj->kzj", pieces, table, precision=mode)


def transform_inverse(spectrum, sine_rows, back_two, back_one, cells_a, cells_b):
    rows_one, depth, length = spectrum.shape
    table = sine_rows.reshape(length, length // cells_b, cells_b)
    pieces = jnp.einsum("kzj,jqc->kqzc", spectrum, table, precision=mode)
    pieces = back_two(pieces.reshape(rows_one, (length // cells_b) * depth * cells_b))
    pieces = pieces.reshape(length, depth, cells_b)
    table = sine_rows.reshape(length, length // cells_a, cells_a)
    volume = jnp.einsum("jzb,jpa->zpab", pieces, table, precision=mode)
    volume = back_one(volume.reshape(depth, (length // cells_a) * cells_a * cells_b))
    volume = volume.reshape(length, cells_a, cells_b)
    return jnp.einsum("kab,kz->abz", volume, sine_rows, precision=mode)


def total_over(values, axis):
    return jnp.sum(lax.all_gather(values, axis), axis=0)


def shards(charge_density):
    cells_a, cells_b, length = charge_density.shape
    tables = [jnp.asarray(table, jnp.float32) for table in build_tables()]
    sine_rows, eigen, basis, select, gather, spread, columns, rows, root, power = tables
    exact = lax.Precision.HIGHEST
    index_x = lax.axis_index("gx")
    index_y = lax.axis_index("gy")

    def swap_one(operand):
        return lax.all_to_all(operand, "gx", split_axis=0, concat_axis=1, tiled=True)

    def swap_two(operand):
        return lax.all_to_all(operand, "gy", split_axis=0, concat_axis=1, tiled=True)

    def back_two(operand):
        return lax.all_to_all(operand, "gy", split_axis=1, concat_axis=0, tiled=True)

    def back_one(operand):
        return lax.all_to_all(operand, "gx", split_axis=1, concat_axis=0, tiled=True)

    count_x = length // lax.axis_size("gy")
    count_z = length // lax.axis_size("gx")
    start_x = index_y * count_x
    start_z = index_x * count_z
    eigen_x = lax.dynamic_slice_in_dim(eigen, start_x, count_x)
    eigen_z = lax.dynamic_slice_in_dim(eigen, start_z, count_z)
    denominator = (
        eigen_x[:, None, None] + eigen_z[None, :, None] + eigen[None, None, :]
    ) * ((length + 1) / 2.0) ** 3
    charge = transform_forward(charge_density, sine_rows, swap_one, swap_two)
    field = charge / denominator

    basis_x = lax.dynamic_slice_in_dim(basis, start_x, count_x)
    basis_z = lax.dynamic_slice_in_dim(basis, start_z, count_z)
    expand_x = jnp.dot(basis_x, select[0], precision=exact)
    expand_y = jnp.dot(basis, select[1], precision=exact)
    expand_z = jnp.dot(basis_z, select[2], precision=exact)
    mixed = jnp.einsum("xzy,ye->xze", field, expand_y, precision=mode)
    entries = jnp.sum(jnp.sum(mixed * expand_z[None], axis=1) * expand_x, axis=0)
    entries = entries.at[ENERGY_LANE].set(jnp.sum(charge * field))
    entries = total_over(total_over(entries, "gx"), "gy")

    owner = np.arange(LANES) // 128
    owner[SPARE:ENERGY_LANE] = 0
    onehot = jnp.asarray(owner[:, None] == np.arange(256)[None, :] // 32, jnp.float32)
    moments = jnp.dot(gather * entries, onehot, precision=exact)
    shape = jnp.sum(moments[:, None, :] * spread, axis=0)

    source = 0.0
    parity = np.arange(length) % 2
    edge = [jnp.where(parity == normal, sine_rows[0], 0.0) for normal in range(2)]
    slab_x = lax.dynamic_slice_in_dim(sine_rows, start_x, count_x)
    slab_z = lax.dynamic_slice_in_dim(sine_rows, start_z, count_z)
    for normal in range(2):
        edge_x = lax.dynamic_slice_in_dim(edge[normal], start_x, count_x)
        edge_z = lax.dynamic_slice_in_dim(edge[normal], start_z, count_z)
        for face in range(3):
            parts = [0.0, 0.0]
            for group in range(8):
                bits = (group >> 2 & 1, group >> 1 & 1, group & 1)
                if face_parity(face, *bits)[2] != normal:
                    continue
                base = group * 32 + face * 9
                right = jnp.dot(shape[:, base : base + 9], columns[base : base + 9], precision=exact)
                parts[sum(bits) % 2] += jnp.dot(rows[group, face].T, right, precision=exact)
            plane = power * (root * parts[0] + parts[1])
            left = (slab_x, slab_z, slab_x)[face]
            half = jnp.dot(left, plane, precision=mode)
            if face == 0:
                full = jnp.dot(half, sine_rows, precision=mode)
                source += full[:, None, :] * edge_z[None, :, None]
            elif face == 1:
                full = jnp.dot(half, sine_rows, precision=mode)
                source += full[None, :, :] * edge_x[:, None, None]
            else:
                full = jnp.dot(half, slab_z.T, precision=mode)
                source += full[:, :, None] * edge[normal][None, None, :]
    total = field + source / denominator
    potential = transform_inverse(total, sine_rows, back_two, back_one, cells_a, cells_b)
    second = total_over(total_over(jnp.sum(charge * total), "gx"), "gy")
    spacing = 1.0 / (length + 1)
    scale = spacing**3
    energies = jnp.stack([scale * entries[ENERGY_LANE], scale * second])
    return potential, energies


def solution(mesh):
    return jax.shard_map(
        shards,
        mesh=mesh,
        in_specs=(P("gx", "gy", None),),
        out_specs=(P("gx", "gy", None), P()),
        check_vma=False,
    )
```

time: 507 us -> 244 us (0.48); the launches traced: 501 us -> 243 us
  matrix products: 124 us -> 44.5 us
  loops' own time: 68 us -> 0 us
  starting transfers between devices: 54.7 us -> 22.2 us
  waiting for transfers between devices: 47.2 us -> 16.5 us
  blocking collectives: 157 us -> 136 us
  other arithmetic: 18.8 us -> 2.95 us
  local copies, waits for them, and re-layouts: 27.8 us -> 18.7 us
    psum x10 -> x0, blocking collectives: 133 us -> none  [over_axes(): x = lax.psum(x, axis)]
    dot_general x222 -> x70, matrix products: 124 us -> 44.5 us  [the longest x1 14.6 us: transform_inverse(): volume = jnp.einsum('jzb,jpa->zpab', pieces, table, precision=mode)]
    unnamed x0 -> x2, blocking collectives: none -> 69.3 us
    another operation x8 -> x0, loops' own time: 68 us -> none  [the longest x4 35 us: shards(): face_terms = lax.cond(owning, moments_of, no_moments, points)]
    all_gather x0 -> x2, blocking collectives: none -> 55.9 us  [total_over(): return jnp.sum(lax.all_gather(values, axis), axis=0)]
    all_to_all x6 -> x3, starting transfers between devices: 54.7 us -> 22.2 us  [the longest x1 11.7 us: swap_one(): lax.all_to_all(operand, 'gx', split_axis=0, concat_axis=1, tiled=True)]
    all_to_all x6 -> x3, waiting for transfers between devices: 47.2 us -> 16.5 us  [the longest x1 10.1 us: swap_one(): lax.all_to_all(operand, 'gx', split_axis=0, concat_axis=1, tiled=True)]
    all_to_all x2 -> x1, blocking collectives: 23.7 us -> 10.6 us  [back_two(): lax.all_to_all(operand, 'gy', split_axis=1, concat_axis=0, tiled=True)]
  transfers between devices with their start and end apart: 6 -> 3, of which waited for: 6 -> 2; matrix products, arithmetic and copies ran while one was open for 1% -> 3% of each run, Pallas kernels for 0% -> 0%
where the time goes in v1:
time: 244 us; the launch traced here: 243 us
  blocking collectives  136 us (56%)
  matrix products  44.5 us (18%)
  starting transfers between devices  22.2 us (9%)
  local copies, waits for them, and re-layouts  18.7 us (8%)
  waiting for transfers between devices  16.5 us (7%)
  other arithmetic  2.95 us (1%)
  between operations  2.69 us (1%)
    unnamed x2, blocking collectives  69.3 us
    all_gather x2, blocking collectives, total_over(): return jnp.sum(lax.all_gather(values, axis), axis=0)  55.9 us
    dot_general x1, matrix products, transform_inverse(): volume = jnp.einsum('jzb,jpa->zpab', pieces, table, precision=mode)  14.6 us
    all_to_all x1, starting transfers between devices, swap_one(): lax.all_to_all(operand, 'gx', split_axis=0, concat_axis=1, tiled=True)  11.7 us
    all_to_all x1, blocking collectives, back_two(): lax.all_to_all(operand, 'gy', split_axis=1, concat_axis=0, tiled=True)  10.6 us
    dot_general x24, matrix products, shards(): parts[sum(bits) % 2] += jnp.dot(rows[group, face].T, right, precision=exact)  10.2 us
    all_to_all x1, waiting for transfers between devices, swap_one(): lax.all_to_all(operand, 'gx', split_axis=0, concat_axis=1, tiled=True)  10.1 us
    all_to_all x1, starting transfers between devices, swap_two(): lax.all_to_all(operand, 'gy', split_axis=0, concat_axis=1, tiled=True)  6.74 us
  transfers between devices with their start and end apart: 3, of which 2 were waited for; matrix products, arithmetic and copies ran while one was open for 3% of the time, Pallas kernels for 0%

profile of v1, /device:TPU:1, one launch (start us, length us, event | category | flops | bytes accessed | tf_op | source)
XLA Modules:
  0.0 243.4 jit_solution(8501157099808171731)
XLA Ops:
  0.6 0.9 copy-done
  1.6 1.2 fusion.114
  3.5 1.7 copy.52
  5.2 11.7 %all-to-all-start = ((f32[16,16,256]{2,1,0:T(8,128)}), f32[16,16,256]{2,1,0:T(8,128)S(1)}, u32[]{:S(2)}, u32[]{:S(2)}) async-start(f32[16,16,256]{2,1,0:T(8,128)} %copy.52), calls=%async_computation | async-start | bytes 524288 | tf_op jit(solution)/shard_map/all_to_all | solution.py:196
  17.1 10.1 %all-to-all-done = f32[16,16,256]{2,1,0:T(8,128)S(1)} async-done(((f32[16,16,256]{2,1,0:T(8,128)}), f32[16,16,256]{2,1,0:T(8,128)S(1)}, u32[]{:S(2)}, u32[]{:S(2)}) %all-to-all-start) | async-done | bytes 262176 | tf_op jit(solution)/shard_map/all_to_all | solution.py:196
  27.9 1.6 convolution_bitcast_fusion.2
  30.1 1.7 copy.53
  31.9 6.7 %all-to-all-start.1 = ((f32[16,16,256]{2,1,0:T(8,128)}), f32[16,16,256]{2,1,0:T(8,128)S(1)}, u32[]{:S(2)}, u32[]{:S(2)}) async-start(f32[16,16,256]{2,1,0:T(8,128)} %copy.53), calls=%async_computation.1 | async-start | bytes 524288 | tf_op jit(solution)/shard_map/all_to_all | solution.py:199
  39.6 6.4 %all-to-all-done.1 = f32[16,16,256]{2,1,0:T(8,128)S(1)} async-done(((f32[16,16,256]{2,1,0:T(8,128)}), f32[16,16,256]{2,1,0:T(8,128)S(1)}, u32[]{:S(2)}, u32[]{:S(2)}) %all-to-all-start.1) | async-done | bytes 262176 | tf_op jit(solution)/shard_map/all_to_all | solution.py:199
  46.8 2.7 %multiply_reduce_fusion.2 = (f32[]{:T(128)}, f32[16,16,256]{2,1,0:T(8,128)S(1)}) fusion(f32[256]{0:T(256)S(1)} %copy-done.22, f32[16,16]{1,0:T(8,128)S(1)} %broadcast_add_fusion, f32[16,16,16,16]{3,2,1,0:T(8,128)S(1)} %reshape.127, f32[16,16,256,1]{2,1,0,3:T(8,128)} %constant.197), kind=kOutput, calls=%fused_computation.46 | convolution fusion | flops 100990976 | bytes 788484 | tf_op jit(solution)/shard_map/kqzc,qcj->kzj/dot_general | solution.py:167
  52.1 32.2 %all-gather.1 = f32[16,1,1024]{2,1,0:T(1,128)S(1)} all-gather(f32[1,1,1024]{2,1,0:T(1,128)S(1)} %scatter.6), channel_id=1, replica_groups=mesh['gx'=16,'gy'=16] {'gx'}, dimensions={0}, use_global_device_ids=true | all-gather | bytes 69632 | tf_op jit(solution)/shard_map/all_gather | solution.py:184
  84.3 23.8 %all-gather = f32[16384]{0:T(1024)S(1)} all-gather(f32[1024]{0:T(1024)S(1)} %reduce_sum.84), channel_id=2, replica_groups=mesh['gx'=16,'gy'=16] {'gy'}, dimensions={0}, use_global_device_ids=true | all-gather | bytes 69632 | tf_op jit(solution)/shard_map/all_gather | solution.py:184
  126.8 1.1 convolution_bitcast_fusion
  127.9 0.9 all_to_all.54
  129.2 10.6 %all_to_all.64 = f32[16,16,256]{2,0,1:T(8,128)S(1)} all-to-all(f32[16,16,256]{2,0,1:T(8,128)S(1)} %copy.43), channel_id=1, replica_groups=mesh['gx'=16,'gy'=16] {'gy'}, dimensions={1} | all-to-all | bytes 524288 | tf_op jit(solution)/shard_map/all_to_all | solution.py:202
  140.5 14.6 %fusion.4 = f32[16,16,16,16]{2,3,1,0:T(8,128)} fusion(f32[256,16,16,1]{0,2,1,3:T(8,128)S(1)} %copy-done.17, f32[256,16,16,1]{2,1,0,3:T(8,128)S(1)} %bitcast.146), kind=kOutput, calls=%fused_computation.4 | convolution fusion | flops 100663296 | bytes 786432 | tf_op jit(solution)/shard_map/jzb,jpa->zpab/dot_general | solution.py:177
  155.1 1.9 copy.56
  157.1 1.5 reshape.159
  158.6 3.7 %all-to-all-start.3 = ((f32[16,16,256]{2,0,1:T(8,128)}), f32[16,16,256]{2,0,1:T(8,128)S(1)}, u32[]{:S(2)}, u32[]{:S(2)}) async-start(f32[16,16,256]{2,0,1:T(8,128)} %reshape.159), calls=%async_computation.3 | async-start | bytes 524288 | tf_op jit(solution)/shard_map/all_to_all | solution.py:205
  165.6 1.3 dynamic-update-slice.3
  166.9 34.9 %all-reduce = f32[16]{0:T(128)S(1)} all-reduce(f32[16]{0:T(128)S(1)} %dynamic-update-slice.3), channel_id=1, replica_groups=mesh['gx'=16,'gy'=16] {'gx'}, use_global_device_ids=true, to_apply=%add | all-reduce | flops 16 | bytes 128
  202.5 1.4 dynamic-update-slice.4
  203.8 34.4 %all-reduce.1 = f32[16]{0:T(128)S(1)} all-reduce(f32[16]{0:T(128)S(1)} %dynamic-update-slice.4), channel_id=1, replica_groups=mesh['gx'=16,'gy'=16] {'gy'}, use_global_device_ids=true, to_apply=%add.1 | all-reduce | flops 16 | bytes 128
  240.7 2.6 %fusion.2 = f32[16,16,256]{2,1,0:T(8,128)} fusion(f32[256,256,1]{1,0,2:T(8,128)S(1)} %copy-done.16, f32[256,16,16]{2,1,0:T(8,128)S(1)} %reshape.130), kind=kOutput, calls=%fused_computation.2 | convolution fusion | flops 100663296 | bytes 786432 | tf_op jit(solution)/shard_map/kab,kz->abz/dot_general | solution.py:180
  (145 shorter events, 30.8 us)
Async XLA Ops:
  2.8 14.1 %copy-start.22 = (f32[256]{0:T(256)S(1)}, f32[256]{0:T(256)}, u32[]{:S(2)}) copy-start(f32[256]{0:T(256)} %constant.72.clone) | copy-start | bytes 3076
  3.5 24.4 %copy-start.18 = (f32[16,16,256,1]{2,0,1,3:T(8,128)S(1)}, f32[16,16,256,1]{2,0,1,3:T(8,128)}, u32[]{:S(2)}) copy-start(f32[16,16,256,1]{2,0,1,3:T(8,128)} %constant.194) | copy-start | bytes 786436
  5.2 22.0 %all-to-all-start = ((f32[16,16,256]{2,1,0:T(8,128)}), f32[16,16,256]{2,1,0:T(8,128)S(1)}, u32[]{:S(2)}, u32[]{:S(2)}) async-start(f32[16,16,256]{2,1,0:T(8,128)} %copy.52), calls=%async_computation | async-start | bytes 524288 | tf_op jit(solution)/shard_map/all_to_all | solution.py:196
  29.5 9.1 %copy-start.23 = (f32[256]{0:T(256)S(1)}, f32[256]{0:T(256)}, u32[]{:S(2)}) copy-start(f32[256]{0:T(256)} %constant.143) | copy-start | bytes 3076
  29.5 9.1 %copy-start.24 = (f32[256]{0:T(256)S(1)}, f32[256]{0:T(256)}, u32[]{:S(2)}) copy-start(f32[256]{0:T(256)} %constant.106) | copy-start | bytes 3076
  29.5 9.2 %copy-start.21 = (f32[32,1024]{1,0:T(8,128)S(1)}, f32[32,1024]{1,0:T(8,128)}, u32[]{:S(2)}) copy-start(f32[32,1024]{1,0:T(8,128)} %constant.89) | copy-start | bytes 393220
  31.9 14.1 %all-to-all-start.1 = ((f32[16,16,256]{2,1,0:T(8,128)}), f32[16,16,256]{2,1,0:T(8,128)S(1)}, u32[]{:S(2)}, u32[]{:S(2)}) async-start(f32[16,16,256]{2,1,0:T(8,128)} %copy.53), calls=%async_computation.1 | async-start | bytes 524288 | tf_op jit(solution)/shard_map/all_to_all | solution.py:199
  46.8 61.3 %copy-start.4 = (f32[1024,256]{1,0:T(8,128)S(1)}, f32[1024,256]{1,0:T(8,128)}, u32[]{:S(2)}) copy-start(f32[1024,256]{1,0:T(8,128)} %constant.81.clone) | copy-start | bytes 3145732
  49.5 58.6 %copy-start.19 = (f32[48,1024]{1,0:T(8,128)S(1)}, f32[48,1024]{1,0:T(8,128)}, u32[]{:S(2)}) copy-start(f32[48,1024]{1,0:T(8,128)} %constant.75.clone) | copy-start | bytes 589828
  49.5 59.3 %copy-start.7 = (f32[48,16,256]{2,1,0:T(8,128)S(1)}, f32[48,16,256]{2,1,0:T(8,128)}, u32[]{:S(2)}) copy-start(f32[48,16,256]{2,1,0:T(8,128)} %constant.76.clone) | copy-start | bytes 2359300
  49.5 59.4 %copy-start.13 = (f32[9,256]{1,0:T(8,128)S(1)}, f32[9,256]{1,0:T(8,128)}, u32[]{:S(2)}) copy-start(f32[9,256]{1,0:T(8,128)} %constant.98) | copy-start | bytes 27652
  49.5 59.8 %copy-start.15 = (f32[9,256]{1,0:T(8,128)S(1)}, f32[9,256]{1,0:T(8,128)}, u32[]{:S(2)}) copy-start(f32[9,256]{1,0:T(8,128)} %constant.101) | copy-start | bytes 27652
  49.6 60.2 %copy-start.14 = (f32[9,256]{1,0:T(8,128)S(1)}, f32[9,256]{1,0:T(8,128)}, u32[]{:S(2)}) copy-start(f32[9,256]{1,0:T(8,128)} %constant.95) | copy-start | bytes 27652
  49.6 60.7 %copy-start.12 = (f32[9,256]{1,0:T(8,128)S(1)}, f32[9,256]{1,0:T(8,128)}, u32[]{:S(2)}) copy-start(f32[9,256]{1,0:T(8,128)} %constant.92) | copy-start | bytes 27652
  50.3 63.5 %copy-start.11 = (f32[16,256]{1,0:T(8,128)S(1)}, f32[16,256]{1,0:T(8,128)}, u32[]{:S(2)}) copy-start(f32[16,256]{1,0:T(8,128)} %constant.94) | copy-start | bytes 49156
  50.4 64.0 %copy-start.9 = (f32[16,256]{1,0:T(8,128)S(1)}, f32[16,256]{1,0:T(8,128)}, u32[]{:S(2)}) copy-start(f32[16,256]{1,0:T(8,128)} %constant.100) | copy-start | bytes 49156
  51.3 63.5 %copy-start.1 = (f32[256,256]{1,0:T(8,128)S(1)}, f32[256,256]{1,0:T(8,128)}, u32[]{:S(2)}) copy-start(f32[256,256]{1,0:T(8,128)} %constant.169) | copy-start | bytes 786436
  51.3 63.5 %copy-start.10 = (f32[16,256]{1,0:T(8,128)S(1)}, f32[16,256]{1,0:T(8,128)}, u32[]{:S(2)}) copy-start(f32[16,256]{1,0:T(8,128)} %constant.97) | copy-start | bytes 49156
  108.1 7.1 %copy-start.2 = (f32[256,256]{1,0:T(8,128)S(1)}, f32[256,256]{1,0:T(8,128)}, u32[]{:S(2)}) copy-start(f32[256,256]{1,0:T(8,128)} %constant.175) | copy-start | bytes 786436
  108.2 7.1 %copy-start.8 = (f32[16,256]{1,0:T(8,128)S(1)}, f32[16,256]{1,0:T(8,128)}, u32[]{:S(2)}) copy-start(f32[16,256]{1,0:T(8,128)} %constant.103) | copy-start | bytes 49156
  108.8 6.8 %copy-start.3 = (f32[256,256]{1,0:T(8,128)S(1)}, f32[256,256]{1,0:T(8,128)}, u32[]{:S(2)}) copy-start(f32[256,256]{1,0:T(8,128)} %constant.71.clone) | copy-start | bytes 786436
  157.1 5.9 %copy-start.26 = (u32[256]{0:T(256)S(1)}, u32[256]{0:T(256)}, u32[]{:S(2)}) copy-start(u32[256]{0:T(256)} %constant.183) | copy-start | bytes 3076
  158.6 82.1 %copy-start.16 = (f32[256,256,1]{1,0,2:T(8,128)S(1)}, f32[256,256,1]{1,0,2:T(8,128)}, u32[]{:S(2)}) copy-start(f32[256,256,1]{1,0,2:T(8,128)} %constant.195) | copy-start | bytes 786436
  158.6 81.5 %all-to-all-start.3 = ((f32[16,16,256]{2,0,1:T(8,128)}), f32[16,16,256]{2,0,1:T(8,128)S(1)}, u32[]{:S(2)}, u32[]{:S(2)}) async-start(f32[16,16,256]{2,0,1:T(8,128)} %reshape.159), calls=%async_computation.3 | async-start | bytes 524288 | tf_op jit(solution)/shard_map/all_to_all | solution.py:205
  (7 other events, 19.3 us)

commit v2 on v1

v2 whole, which is shorter than its diff:
```python
import math

import jax
import jax.numpy as jnp
import numpy as np
from jax import lax
from jax.experimental import pallas as pl
from jax.experimental.pallas import tpu as pltpu
from jax.sharding import PartitionSpec as P

ORDER = 16
N = 256
SLOTS = 48
LANES = 1024
SPARE = 7 * 128 + 112
ENERGY_LANE = 1023


def harmonics(x, y, z):
    cosine = {(0, 0): np.ones_like(x)}
    sine = {(0, 0): np.zeros_like(x)}
    for l in range(1, ORDER + 1):
        scale = 1.0 if l == 1 else math.sqrt((2 * l - 1) / (2.0 * l))
        c, s = cosine[l - 1, l - 1], sine[l - 1, l - 1]
        cosine[l, l] = scale * (x * c - y * s)
        sine[l, l] = scale * (x * s + y * c)
        for m in range(l):
            near = (2 * l - 1) / math.sqrt(l * l - m * m)
            far = math.sqrt((l - 1) ** 2 - m * m) / math.sqrt(l * l - m * m)
            for table in (cosine, sine):
                older = table[l - 2, m] if l - 2 >= m else 0.0
                table[l, m] = near * z * table[l - 1, m] - far * older
    return cosine, sine


def face_point(face, t, s):
    one = np.ones_like(t)
    return ((s, t, one), (s, one, t), (one, t, s))[face]


def face_parity(face, px, py, pz):
    return ((py, px, pz), (pz, px, py), (py, pz, px))[face]


def trig(parity, odd, angle):
    if odd:
        orders = np.arange(1, 16, 2)
    else:
        orders = np.arange(0, 17, 2) if parity == 0 else np.arange(2, 17, 2)
    wave = np.cos if parity == 0 else np.sin
    return wave(orders[:, None] * angle[None, :])


def build_tables():
    span = N + 1.0
    step = 1.0 / span
    radius = math.sqrt(3.0) / 2.0
    index = np.arange(N) + 1
    sine_rows = np.sin(np.pi * (index[:, None] * index[None, :] % (2 * N + 2)) / span)
    eigen = 4.0 * span * span * np.sin(np.pi * index / (2 * span)) ** 2
    scaled = 2.0 * (np.arange(N) - (N - 1) / 2.0) * step
    angle = np.arctan(scaled)

    terms = [[] for _ in range(8)]
    for l in range(ORDER + 1):
        for m in range(l + 1):
            terms[(m % 2) * 4 + (l - m) % 2].append((l, m, 0))
            if m:
                terms[((m - 1) % 2) * 4 + 2 + (l - m) % 2].append((l, m, 1))

    nodes, quad = np.polynomial.legendre.leggauss(24)
    legendre = np.polynomial.legendre.legvander(nodes, ORDER).T
    basis = np.zeros((N, 32))
    basis[:, : ORDER + 1] = sine_rows @ np.polynomial.legendre.legvander(scaled, ORDER)
    even = (np.arange(N) % 2 == 0).astype(np.float64)
    basis[:, 17] = sine_rows[0] * even
    basis[:, 18] = sine_rows[0] * (1.0 - even)
    project = legendre * quad[None, :] * (np.arange(ORDER + 1) + 0.5)[:, None]
    turns = 64
    circle = 2.0 * np.pi * np.arange(turns) / turns
    ones_t, ones_s = np.meshgrid(nodes, nodes, indexing="ij")
    alpha, beta = np.meshgrid(circle, circle, indexing="ij")
    solid, wave = [], []
    for face in range(3):
        x, y, z = face_point(face, ones_t, ones_s)
        r = np.sqrt(x * x + y * y + z * z)
        table = harmonics(x / r, y / r, z / r)
        solid.append((table, r / math.sqrt(3.0)))
        ca, sa, cb, sb = np.cos(alpha), np.sin(alpha), np.cos(beta), np.sin(beta)
        parts = (sa * cb, ca * sb, ca * cb)
        order = ((1, 0, 2), (1, 2, 0), (2, 0, 1))[face]
        x, y, z = (parts[k] for k in order)
        r = np.sqrt(x * x + y * y + z * z)
        safe = np.where(r < 1e-12, 1.0, r)
        wave.append((harmonics(x / safe, y / safe, z / safe), np.where(r < 1e-12, 0.0, r)))

    select = np.zeros((3, 32, LANES))
    gather = np.zeros((SLOTS, LANES))
    spread = np.zeros((SLOTS, 16, 256))
    columns = np.zeros((256, N))
    rows = np.zeros((8, 3, 16, N))
    spill = SPARE
    for group in range(8):
        px, py, pz = group >> 2 & 1, group >> 1 & 1, group & 1
        odd = (px + py + pz) % 2
        lane = group * 128
        for face in range(3):
            prow, pcol, normal = face_parity(face, px, py, pz)
            sign = 2.0 if normal == 0 else -2.0
            entries = [
                (i, j)
                for i in range(prow, ORDER + 1, 2)
                for j in range(pcol, ORDER + 1, 2)
                if i + j + normal <= ORDER - odd
            ]
            moments = {}
            for slot, (l, m, which) in enumerate(terms[group]):
                table, ratio = solid[face]
                values = ratio**l * table[which][l, m]
                moments[slot] = project @ values @ project.T
            for i, j in entries:
                if lane >= (group + 1) * 128 or (lane >= SPARE and group == 7):
                    position, spill = spill, spill + 1
                    assert group == 0
                else:
                    position, lane = lane, lane + 1
                axes = ((1, 0, 2), (2, 0, 1), (1, 2, 0))[face]
                select[axes[0], i, position] = 1.0
                select[axes[1], j, position] = 1.0
                select[axes[2], 17 + normal, position] = 1.0
                for slot in moments:
                    gather[slot, position] = step * sign * moments[slot][i, j]
            left = trig(prow, odd, circle)
            right = trig(pcol, odd, circle)
            left_unit = left / np.sum(left * left, axis=1, keepdims=True)
            right_unit = right / np.sum(right * right, axis=1, keepdims=True)
            base = group * 32 + face * 9
            for slot, (l, m, which) in enumerate(terms[group]):
                table, r = wave[face]
                values = r ** (ORDER - odd) * table[which][l, m]
                block = left_unit @ values @ right_unit.T
                weight = (1.0 if m == 0 else 2.0) / (4.0 * math.pi * radius * 1.1 ** (l + 1))
                block = block * weight * sign * span * span
                spread[slot, : block.shape[0], base : base + block.shape[1]] = block
            tail = trig(pcol, odd, angle)
            columns[base : base + tail.shape[0]] = tail
            head = trig(prow, odd, angle)
            rows[group, face, : head.shape[0]] = head
    assert spill < ENERGY_LANE
    root = 1.0 / np.sqrt(1.0 - np.outer(np.sin(angle) ** 2, np.sin(angle) ** 2))
    return sine_rows, eigen, basis, select, gather, spread, columns, rows, root, root**15

MESH = pl.DeviceIdType.MESH
SIDE = 16
HALF = 128
F32 = jnp.float32
BF16 = jnp.bfloat16
NN = (((1,), (0,)), ((), ()))
NT = (((1,), (1,)), ((), ()))


def split(value):
    high = value.astype(BF16)
    return high, (value - high.astype(F32)).astype(BF16)


def dot(a, b, dims=NN):
    return lax.dot_general(a, b, dims, preferred_element_type=F32)


def dot3(a, b, dims=NN):
    return dot(a[0], b[0], dims) + (dot(a[0], b[1], dims) + dot(a[1], b[0], dims))


def regroup(load, store, roll):
    lane = lax.broadcasted_iota(jnp.int32, (4 * SIDE, HALF), 1)
    rows = [
        jnp.concatenate([load(8 * a + i, h) for a in range(2) for h in range(2)], axis=0)
        for i in range(8)
    ]
    for step in (4, 2, 1):
        keep = (lane // (SIDE * step)) % 2 == 0
        for i in range(8):
            if i & step == 0:
                one, two = rows[i], rows[i + step]
                rows[i] = jnp.where(keep, one, roll(two, SIDE * step))
                rows[i + step] = jnp.where(keep, roll(one, HALF - SIDE * step), two)
    for i in range(8):
        for a in range(2):
            for h in range(2):
                part = 2 * a + h
                store(8 * h + i, a, rows[i][part * SIDE : (part + 1) * SIDE])


def local_entries(field, expand_x, expand_y, expand_z, energy):
    pieces = split(field)
    outcome = []
    for tile in range(4):
        lanes = slice(tile * 256, (tile + 1) * 256)
        mixed = dot3(pieces, (expand_x[0][:, lanes], expand_x[1][:, lanes]))
        total = mixed[:SIDE] * expand_z[0:1, lanes]
        for k in range(1, SIDE):
            total += mixed[k * SIDE : (k + 1) * SIDE] * expand_z[k : k + 1, lanes]
        summed = jnp.sum(total * expand_y[:, lanes], axis=0, keepdims=True)
        outcome += [summed[:, :HALF], summed[:, HALF:]]
    lane = lax.broadcasted_iota(jnp.int32, (1, HALF), 1)
    outcome[7] = jnp.where(lane == HALF - 1, energy, outcome[7])
    return outcome


def owner_map():
    row = lax.broadcasted_iota(jnp.int32, (LANES, 256), 0)
    lane = lax.broadcasted_iota(jnp.int32, (LANES, 256), 1)
    owner = jnp.where(row >= SPARE, 0, row // HALF)
    return jnp.where(owner == lane // 32, 1.0, 0.0).astype(BF16)


def surface_hats(entries, gather, spread, onehot, columns, heads, root, power, at_y, at_z, sines):
    product = jnp.concatenate(
        [gather[:, r * HALF : (r + 1) * HALF] * entries[r : r + 1, :] for r in range(8)], axis=1
    )
    high, rest = product.astype(BF16), None
    rest = product - high.astype(F32)
    middle = rest.astype(BF16)
    low = (rest - middle.astype(F32)).astype(BF16)
    moments = dot(high, onehot) + (dot(middle, onehot) + dot(low, onehot))
    shape = moments[0:1, :] * spread[0]
    for slot in range(1, 45):
        shape += moments[slot : slot + 1, :] * spread[slot]
    lane = lax.broadcasted_iota(jnp.int32, (SIDE, 256), 1)
    blocks = []
    for face in range(3):
        for normal in range(2):
            for odd in range(2):
                for head in range(2):
                    tail = (odd + normal + head) % 2
                    px, py, pz = (
                        (tail, head, normal),
                        (tail, normal, head),
                        (normal, head, tail),
                    )[face]
                    base = (px * 4 + py * 2 + pz) * 32 + face * 9
                    blocks.append(jnp.where((lane >= base) & (lane < base + 9), shape, 0.0))
    right = dot3(split(jnp.concatenate(blocks, axis=0)), columns)
    hats = []
    for face in range(3):
        left = at_z if face == 1 else at_y
        both = jnp.concatenate(left, axis=0)
        for normal in range(2):
            parts = []
            for odd in range(2):
                start = ((face * 2 + normal) * 2 + odd) * 32
                high, low = split(right[start : start + 32])
                stack = jnp.concatenate([high, low, high, low], axis=0)
                parts.append(dot(heads[odd * 256 : (odd + 1) * 256, :], stack))
            plane = split(power * (root * parts[0] + parts[1]))
            first = dot(both, plane[0])
            hats.append(first[:SIDE] + (first[SIDE:] + dot(left[0], plane[1])))
    full = dot3(split(jnp.concatenate(hats[:4], axis=0)), sines)
    last = dot3(split(jnp.concatenate(hats[4:], axis=0)), at_z, NT)
    return full, last


def source_block(k, full, last, edge_y, edge_z, edge_lane):
    ky = lax.broadcasted_iota(jnp.int32, (SIDE, 256), 0)
    wide = jnp.concatenate([edge_y, edge_y], axis=1)
    scale = edge_z[k : k + 1, :]
    scale = jnp.concatenate([scale, scale], axis=1)
    normal = k % 2
    value = full[normal * SIDE : (normal + 1) * SIDE] * scale
    side = jnp.where(
        ky % 2 == 0,
        full[2 * SIDE + k : 2 * SIDE + k + 1, :],
        full[3 * SIDE + k : 3 * SIDE + k + 1, :],
    )
    value += side * wide
    value += last[:SIDE, k : k + 1] * edge_lane[0] + last[SIDE:, k : k + 1] * edge_lane[1]
    return value


def start_all(phase, source, target, axis, me, send_sem, recv_sem, rows):
    def body(d, carry):
        copy_of(phase, source, target, axis, me, send_sem, recv_sem, rows, d).start()
        return carry

    lax.fori_loop(1, SIDE, body, 0)


def copy_of(phase, source, target, axis, me, send_sem, recv_sem, rows, d):
    peer = lax.rem(me + d, SIDE)
    if rows is None:
        src = source
    else:
        src = source.at[pl.ds(pl.multiple_of(peer * rows, rows), rows), :]
    count = source.shape[0] if rows is None else rows
    return pltpu.make_async_remote_copy(
        src_ref=src,
        dst_ref=target.at[pl.ds(pl.multiple_of(me * count, count), count), :],
        send_sem=send_sem.at[phase, d],
        recv_sem=recv_sem.at[phase, d],
        device_id={axis: peer},
        device_id_type=MESH,
    )


def finish_all(phase, source, target, axis, me, send_sem, recv_sem, rows, sent):
    def body(d, carry):
        copy = copy_of(phase, source, target, axis, me, send_sem, recv_sem, rows, d)
        if sent:
            copy.wait_send()
        else:
            copy.wait_recv()
        return carry

    lax.fori_loop(1, SIDE, body, 0)


def sum_slots(ref):
    total = ref[0:8, :]
    for slot in range(1, SIDE):
        total += ref[slot * 8 : (slot + 1) * 8, :]
    return total


CONSTANTS = 15


def kernel(*refs):
    charge_hbm = refs[0]
    held_hbm = refs[1 : 1 + CONSTANTS]
    out_ref, energy_ref = refs[1 + CONSTANTS : 3 + CONSTANTS]
    scratch = refs[3 + CONSTANTS :]
    charge = scratch[0]
    held = scratch[1 : 1 + CONSTANTS]
    sends = scratch[1 + CONSTANTS : 5 + CONSTANTS]
    lands = scratch[5 + CONSTANTS : 9 + CONSTANTS]
    (
        mats, spectrum, field_ref, inverse_ref, expand_high, expand_low, expand_y, expand_z,
        onehot, small_send, small_land, local_sem, send_sem, recv_sem,
    ) = scratch[9 + CONSTANTS :]
    (
        sine_high, sine_low, eigen_wide, edge_wide, lane_rows, basis_high, basis_low, select,
        gather, spread, column_high, column_low, heads, root, power,
    ) = held
    p = lax.axis_index("gx")
    q = lax.axis_index("gy")

    copies = [pltpu.make_async_copy(charge_hbm, charge, local_sem.at[0])]
    for i in range(CONSTANTS):
        copies.append(pltpu.make_async_copy(held_hbm[i], held[i], local_sem.at[i + 1]))
    for copy in copies:
        copy.start()

    barrier = pltpu.get_barrier_semaphore()

    def greet(d, carry):
        pl.semaphore_signal(
            barrier, inc=1, device_id={"gx": lax.rem(p + d, SIDE)}, device_id_type=MESH
        )
        pl.semaphore_signal(
            barrier, inc=1, device_id={"gy": lax.rem(q + d, SIDE)}, device_id_type=MESH
        )
        return carry

    lax.fori_loop(1, SIDE, greet, 0)

    def at(index):
        return pl.ds(pl.multiple_of(index * SIDE, SIDE), SIDE)

    def sines():
        return sine_high[...], sine_low[...]

    def launch(phase, value, axis, me):
        sends[phase][...] = dot3(sines(), split(value), NT)
        if phase == 0:
            pl.semaphore_wait(barrier, 2 * (SIDE - 1))
        start_all(phase, sends[phase], lands[phase], axis, me, send_sem, recv_sem, SIDE)
        lands[phase][at(me), :] = sends[phase][at(me), :]

    def collect(phase, axis, me, strided):
        finish_all(phase, sends[phase], lands[phase], axis, me, send_sem, recv_sem, SIDE, False)
        land = lands[phase]

        def load(a, h):
            return land[a * SIDE : (a + 1) * SIDE, h * HALF : (h + 1) * HALF]

        def store(g, h, piece):
            if strided:
                mats[h][pl.ds(g, SIDE, stride=SIDE), :] = piece
            else:
                mats[h][g * SIDE : (g + 1) * SIDE, :] = piece

        regroup(load, store, lambda v, amount: pltpu.roll(v, amount, 1))

    def mat():
        return jnp.concatenate([mats[0][...], mats[1][...]], axis=1)

    def small(phase, index, value, axis, me):
        small_send[index][...] = value
        start_all(phase, small_send[index], small_land[index], axis, me, send_sem, recv_sem, None)
        small_land[index][pl.ds(pl.multiple_of(me * 8, 8), 8), :] = value

    def small_total(phase, index, axis, me):
        finish_all(
            phase, small_send[index], small_land[index], axis, me, send_sem, recv_sem, None, False
        )
        return sum_slots(small_land[index])

    copies[0].wait()
    copies[1].wait()
    copies[2].wait()
    launch(0, charge[...], "gy", q)

    for copy in copies[3:]:
        copy.wait()
    for tile in range(4):
        lanes = slice(tile * 256, (tile + 1) * 256)
        expand_high[:, lanes] = dot(basis_high[...], select[0:32, lanes]).astype(BF16)
        expand_low[:, lanes] = dot(basis_low[...], select[0:32, lanes]).astype(BF16)
        expand_y[:, lanes] = dot(basis_high[at(p), :], select[32:64, lanes]) + dot(
            basis_low[at(p), :], select[32:64, lanes]
        )
        expand_z[:, lanes] = dot(basis_high[at(q), :], select[64:96, lanes]) + dot(
            basis_low[at(q), :], select[64:96, lanes]
        )
    eigen_y = eigen_wide[at(p), :]
    eigen_y = jnp.concatenate([eigen_y, eigen_y], axis=1) + lane_rows[0:1, :]
    eigen_z = eigen_wide[at(q), :]
    eigen_z = jnp.concatenate([eigen_z, eigen_z], axis=1)
    cube = ((N + 1) / 2.0) ** 3
    for k in range(SIDE):
        rows = slice(k * SIDE, (k + 1) * SIDE)
        inverse_ref[rows, :] = 1.0 / ((eigen_y + eigen_z[k : k + 1, :]) * cube)
    onehot[...] = owner_map()

    collect(0, "gy", q, True)
    launch(1, mat(), "gx", p)
    collect(1, "gx", p, False)

    value = dot3(split(mat()), sines())
    spectrum[...] = value
    field = value * inverse_ref[...]
    field_ref[...] = field
    energy = jnp.sum(jnp.sum(value * field, axis=1, keepdims=True), axis=0, keepdims=True)
    entries = local_entries(
        field, (expand_high, expand_low), expand_y, expand_z, energy
    )
    small(4, 0, jnp.concatenate(entries, axis=0), "gx", p)
    partial = small_total(4, 0, "gx", p)
    small(5, 1, partial, "gy", q)
    entries = small_total(5, 1, "gy", q)

    at_y = (sine_high[at(p), :], sine_low[at(p), :])
    at_z = (sine_high[at(q), :], sine_low[at(q), :])
    full, last = surface_hats(
        entries, gather, spread, onehot[...], (column_high[...], column_low[...]), heads,
        root[...], power[...], at_y, at_z, sines(),
    )
    edge_y = edge_wide[at(p), :]
    edge_z = edge_wide[at(q), :]
    edge_lane = (lane_rows[1:2, :], lane_rows[2:3, :])
    second = jnp.zeros((SIDE, 256), F32)
    for k in range(SIDE):
        rows = slice(k * SIDE, (k + 1) * SIDE)
        total = field_ref[rows, :] + inverse_ref[rows, :] * source_block(
            k, full, last, edge_y, edge_z, edge_lane
        )
        second += spectrum[rows, :] * total
        mats[0][rows, :] = total[:, :HALF]
        mats[1][rows, :] = total[:, HALF:]
    launch(2, mat(), "gx", p)
    second = jnp.sum(jnp.sum(second, axis=1, keepdims=True), axis=0, keepdims=True)
    small(6, 2, jnp.broadcast_to(second, (8, HALF)), "gx", p)
    collect(2, "gx", p, True)
    launch(3, mat(), "gy", q)
    small(7, 3, small_total(6, 2, "gx", p), "gy", q)
    collect(3, "gy", q, False)
    out_ref[...] = dot3(split(mat()), sines())
    second = small_total(7, 3, "gy", q)
    lane = lax.broadcasted_iota(jnp.int32, (8, HALF), 1)
    first = jnp.broadcast_to(entries[7:8, HALF - 1 :], (8, HALF))
    energy_ref[...] = jnp.where(lane == 0, first, second) * (1.0 / (N + 1)) ** 3

    axes = (("gy", q), ("gx", p), ("gx", p), ("gy", q))
    for phase in range(4):
        axis, me = axes[phase]
        finish_all(phase, sends[phase], lands[phase], axis, me, send_sem, recv_sem, SIDE, True)
    axes = (("gx", p), ("gy", q), ("gx", p), ("gy", q))
    for index in range(4):
        axis, me = axes[index]
        finish_all(
            4 + index, small_send[index], small_land[index], axis, me, send_sem, recv_sem, None, True
        )


def constants():
    sine_rows, eigen, basis, select, gather, spread, columns, rows, root, power = build_tables()

    def pair(table):
        table = table.astype(np.float32)
        high = table.astype(jnp.bfloat16)
        return high, (table - high.astype(np.float32)).astype(jnp.bfloat16)

    parity = np.arange(N) % 2
    lane_rows = np.zeros((8, N))
    lane_rows[0] = eigen
    lane_rows[1] = sine_rows[0] * (parity == 0)
    lane_rows[2] = sine_rows[0] * (parity == 1)
    heads = []
    for odd in range(2):
        tables = [trig(parity_of, odd, np.arctan(2.0 * (np.arange(N) - (N - 1) / 2.0) / (N + 1))) for parity_of in range(2)]
        wide = np.zeros((N, 32))
        for k, table in enumerate(tables):
            wide[:, 16 * k : 16 * k + table.shape[0]] = table.T
        high, low = pair(wide)
        heads.append(np.concatenate([high, high, low, low], axis=1))
    plain = np.float32
    return [
        *pair(sine_rows),
        np.repeat(eigen[:, None], HALF, 1).astype(plain),
        np.repeat(sine_rows[0][:, None], HALF, 1).astype(plain),
        lane_rows.astype(plain),
        *pair(basis),
        np.concatenate(list(select), axis=0).astype(jnp.bfloat16),
        gather.astype(plain),
        spread.astype(plain),
        *pair(columns),
        np.concatenate(heads, axis=0),
        root.astype(plain),
        power.astype(plain),
    ]


def solution(mesh):
    tables = constants()

    def shards(charge_density):
        cells_a, cells_b, length = charge_density.shape
        flat = charge_density.reshape(cells_a * cells_b, length)
        grid = pltpu.VMEM((256, 256), F32)
        hold = [pltpu.VMEM(table.shape, table.dtype) for table in tables]
        potential, energies = pl.pallas_call(
            kernel,
            out_shape=(
                jax.ShapeDtypeStruct((256, 256), F32),
                jax.ShapeDtypeStruct((8, HALF), F32),
            ),
            in_specs=[pl.BlockSpec(memory_space=pl.ANY)] * (1 + CONSTANTS),
            out_specs=(
                pl.BlockSpec(memory_space=pltpu.VMEM),
                pl.BlockSpec(memory_space=pltpu.VMEM),
            ),
            scratch_shapes=[
                grid,
                *hold,
                *[grid] * 8,
                [pltpu.VMEM((256, HALF), F32)] * 2,
                *[grid] * 3,
                pltpu.VMEM((256, LANES), BF16),
                pltpu.VMEM((256, LANES), BF16),
                pltpu.VMEM((SIDE, LANES), F32),
                pltpu.VMEM((SIDE, LANES), F32),
                pltpu.VMEM((LANES, 256), BF16),
                [pltpu.VMEM((8, HALF), F32)] * 4,
                [pltpu.VMEM((8 * SIDE, HALF), F32)] * 4,
                pltpu.SemaphoreType.DMA((1 + CONSTANTS,)),
                pltpu.SemaphoreType.DMA((8, SIDE)),
                pltpu.SemaphoreType.DMA((8, SIDE)),
            ],
            compiler_params=pltpu.CompilerParams(
                collective_id=0, has_side_effects=True, vmem_limit_bytes=48 * 1024 * 1024
            ),
        )(flat, *[jnp.asarray(table) for table in tables])
        return potential.reshape(cells_a, cells_b, length), energies[0, :2]

    return jax.shard_map(
        shards,
        mesh=mesh,
        in_specs=(P("gx", "gy", None),),
        out_specs=(P("gx", "gy", None), P()),
        check_vma=False,
    )
```

time: 244 us -> 79.3 us (0.33)
  blocking collectives: 136 us -> 0 us
  Pallas kernels: 0 us -> 62.3 us
  matrix products: 44.5 us -> 0 us
  starting transfers between devices: 22.2 us -> 0 us
  waiting for transfers between devices: 16.5 us -> 0 us
  local copies, waits for them, and re-layouts: 18.7 us -> 15.7 us
  other arithmetic: 2.95 us -> 0 us
    unnamed x2 -> x0, blocking collectives: 69.3 us -> none
    pallas_call x0 -> x1, Pallas kernels: none -> 62.3 us  [shards(): pl.pallas_call(kernel, out_shape=(jax.ShapeDtypeStruct((256, 256), F32),...]
    all_gather x2 -> x0, blocking collectives: 55.9 us -> none  [total_over(): return jnp.sum(lax.all_gather(values, axis), axis=0)]
    dot_general x70 -> x0, matrix products: 44.5 us -> none  [the longest x1 14.6 us: transform_inverse(): volume = jnp.einsum('jzb,jpa->zpab', pieces, table, precision=mode)]
    all_to_all x3 -> x0, starting transfers between devices: 22.2 us -> none  [the longest x1 11.7 us: swap_one(): lax.all_to_all(operand, 'gx', split_axis=0, concat_axis=1, tiled=True)]
    all_to_all x3 -> x0, waiting for transfers between devices: 16.5 us -> none  [the longest x1 10.1 us: swap_one(): lax.all_to_all(operand, 'gx', split_axis=0, concat_axis=1, tiled=True)]
    all_to_all x1 -> x0, blocking collectives: 10.6 us -> none  [back_two(): lax.all_to_all(operand, 'gy', split_axis=1, concat_axis=0, tiled=True)]
    all_to_all x10 -> x0, local copies, waits for them, and re-layouts: 10.2 us -> none  [the longest x2 3.47 us: back_one(): lax.all_to_all(operand, 'gx', split_axis=1, concat_axis=0, tiled=True)]
  transfers between devices with their start and end apart: 3 -> 0, of which waited for: 2 -> 0; matrix products, arithmetic and copies ran while one was open for 3% -> 0% of each run, Pallas kernels for 0% -> 0%
where the time goes in v2:
time: 79.3 us; the launch traced here: 78.7 us
  Pallas kernels  62.3 us (79%)
  local copies, waits for them, and re-layouts  15.7 us (20%)
    pallas_call x1, Pallas kernels, shards(): pl.pallas_call(kernel, out_shape=(jax.ShapeDtypeStruct((256, 256), F32),...  62.3 us
    unnamed x33, local copies, waits for them, and re-layouts  15.2 us

profile of v2, /device:TPU:1, one launch (start us, length us, event | category | flops | bytes accessed | tf_op | source)
XLA Modules:
  0.0 78.7 jit_solution(17754152223154701169)
XLA Ops:
  0.6 0.0 copy-start.15
  0.6 0.7 copy-done.15
  1.3 0.0 copy-start
  1.3 1.1 %copy-done = f32[48,16,256]{2,1,0:T(8,128)S(1)} copy-done((f32[48,16,256]{2,1,0:T(8,128)S(1)}, f32[48,16,256]{2,1,0:T(8,128)}, u32[]{:S(2)}) %copy-start) | copy-done | bytes 786456
  2.5 0.0 copy-start.1
  2.5 0.9 %copy-done.1 = f32[16,16,256]{2,1,0:T(8,128)S(1)} copy-done((f32[16,16,256]{2,1,0:T(8,128)S(1)}, f32[16,16,256]{2,1,0:T(8,128)}, u32[]{:S(2)}) %copy-start.1) | copy-done | bytes 262168
  3.4 0.0 copy-start.2
  3.4 0.9 %copy-done.2 = f32[256,256]{1,0:T(8,128)S(1)} copy-done((f32[256,256]{1,0:T(8,128)S(1)}, f32[256,256]{1,0:T(8,128)}, u32[]{:S(2)}) %copy-start.2) | copy-done | bytes 262168
  4.4 0.0 copy-start.3
  4.4 0.9 %copy-done.3 = f32[256,256]{1,0:T(8,128)S(1)} copy-done((f32[256,256]{1,0:T(8,128)S(1)}, f32[256,256]{1,0:T(8,128)}, u32[]{:S(2)}) %copy-start.3) | copy-done | bytes 262168
  5.3 0.9 %copy-done.4 = f32[48,1024]{1,0:T(8,128)S(1)} copy-done((f32[48,1024]{1,0:T(8,128)S(1)}, f32[48,1024]{1,0:T(8,128)}, u32[]{:S(2)}) %copy-start.4) | copy-done | bytes 196632
  6.2 0.9 %copy-done.5 = bf16[96,1024]{1,0:T(8,128)(2,1)S(1)} copy-done((bf16[96,1024]{1,0:T(8,128)(2,1)S(1)}, bf16[96,1024]{1,0:T(8,128)(2,1)}, u32[]{:S(2)}) %copy-start.5) | copy-done | bytes 196632
  7.2 0.9 %copy-done.6 = bf16[512,128]{1,0:T(8,128)(2,1)S(1)} copy-done((bf16[512,128]{1,0:T(8,128)(2,1)S(1)}, bf16[512,128]{1,0:T(8,128)(2,1)}, u32[]{:S(2)}) %copy-start.6) | copy-done | bytes 131096
  8.1 0.9 %copy-done.7 = bf16[256,256]{1,0:T(8,128)(2,1)S(1)} copy-done((bf16[256,256]{1,0:T(8,128)(2,1)S(1)}, bf16[256,256]{1,0:T(8,128)(2,1)}, u32[]{:S(2)}) %copy-start.7) | copy-done | bytes 131096
  9.0 0.9 %copy-done.8 = bf16[256,256]{1,0:T(8,128)(2,1)S(1)} copy-done((bf16[256,256]{1,0:T(8,128)(2,1)S(1)}, bf16[256,256]{1,0:T(8,128)(2,1)}, u32[]{:S(2)}) %copy-start.8) | copy-done | bytes 131096
  9.9 0.9 %copy-done.9 = f32[256,128]{1,0:T(8,128)S(1)} copy-done((f32[256,128]{1,0:T(8,128)S(1)}, f32[256,128]{1,0:T(8,128)}, u32[]{:S(2)}) %copy-start.9) | copy-done | bytes 131096
  10.8 0.9 %copy-done.10 = f32[256,128]{1,0:T(8,128)S(1)} copy-done((f32[256,128]{1,0:T(8,128)S(1)}, f32[256,128]{1,0:T(8,128)}, u32[]{:S(2)}) %copy-start.10) | copy-done | bytes 131096
  11.7 0.9 %copy-done.11 = bf16[256,256]{1,0:T(8,128)(2,1)S(1)} copy-done((bf16[256,256]{1,0:T(8,128)(2,1)S(1)}, bf16[256,256]{1,0:T(8,128)(2,1)}, u32[]{:S(2)}) %copy-start.11) | copy-done | bytes 131096
  12.6 0.9 %copy-done.12 = bf16[256,256]{1,0:T(8,128)(2,1)S(1)} copy-done((bf16[256,256]{1,0:T(8,128)(2,1)S(1)}, bf16[256,256]{1,0:T(8,128)(2,1)}, u32[]{:S(2)}) %copy-start.12) | copy-done | bytes 131096
  13.5 0.8 %copy-done.13 = bf16[256,32]{1,0:T(8,128)(2,1)S(1)} copy-done((bf16[256,32]{1,0:T(8,128)(2,1)S(1)}, bf16[256,32]{1,0:T(8,128)(2,1)}, u32[]{:S(2)}) %copy-start.13) | copy-done | bytes 16408
  14.3 0.8 %copy-done.14 = bf16[256,32]{1,0:T(8,128)(2,1)S(1)} copy-done((bf16[256,32]{1,0:T(8,128)(2,1)S(1)}, bf16[256,32]{1,0:T(8,128)(2,1)}, u32[]{:S(2)}) %copy-start.14) | copy-done | bytes 16408
  15.2 62.3 %shard_map.167 = (f32[256,256]{1,0:T(8,128)S(1)}, f32[8,128]{1,0:T(8,128)S(1)}) custom-call(f32[256,256]{1,0:T(8,128)S(1)} %bitcast.4, bf16[256,256]{1,0:T(8,128)(2,1)S(1)} %copy-done.12, bf16[256,256]{1,0:T(8,128)(2,1)S(1)} %copy-done.11, f32[256,128]{1,0:T(8,128)S(1)} %copy-done.10, f32[256,128]{1,0:T(8,128)S(1)} %copy-done.9, f32[8,256]{1,0:T(8,128)S(1)} %copy-done.15, ...), custom_call_target="tpu_custom_call" | custom-call | tf_op jit(solution)/shard_map/pallas_call | solution.py:542
  77.5 0.5 slice_bitcast_fusion
  78.0 0.7 copy.19
  (11 shorter events, 0.0 us)
Async XLA Ops:
  0.6 0.7 copy-start.15
  1.3 1.1 %copy-start = (f32[48,16,256]{2,1,0:T(8,128)S(1)}, f32[48,16,256]{2,1,0:T(8,128)}, u32[]{:S(2)}) copy-start(f32[48,16,256]{2,1,0:T(8,128)} %constant.39.clone.refs_10_) | copy-start | bytes 2359300
  2.5 0.9 %copy-start.1 = (f32[16,16,256]{2,1,0:T(8,128)S(1)}, f32[16,16,256]{2,1,0:T(8,128)}, u32[]{:S(2)}) copy-start(f32[16,16,256]{2,1,0:T(8,128)} %param.16) | copy-start | bytes 786436
  3.4 0.9 %copy-start.2 = (f32[256,256]{1,0:T(8,128)S(1)}, f32[256,256]{1,0:T(8,128)}, u32[]{:S(2)}) copy-start(f32[256,256]{1,0:T(8,128)} %constant.44.clone.refs_15_) | copy-start | bytes 786436
  4.4 0.9 %copy-start.3 = (f32[256,256]{1,0:T(8,128)S(1)}, f32[256,256]{1,0:T(8,128)}, u32[]{:S(2)}) copy-start(f32[256,256]{1,0:T(8,128)} %constant.43.clone.refs_14_) | copy-start | bytes 786436
  5.3 0.9 %copy-start.4 = (f32[48,1024]{1,0:T(8,128)S(1)}, f32[48,1024]{1,0:T(8,128)}, u32[]{:S(2)}) copy-start(f32[48,1024]{1,0:T(8,128)} %constant.38.clone.refs_9_) | copy-start | bytes 589828
  6.2 0.9 %copy-start.5 = (bf16[96,1024]{1,0:T(8,128)(2,1)S(1)}, bf16[96,1024]{1,0:T(8,128)(2,1)}, u32[]{:S(2)}) copy-start(bf16[96,1024]{1,0:T(8,128)(2,1)} %constant.37.clone.refs_8_) | copy-start | bytes 589828
  7.2 0.9 %copy-start.6 = (bf16[512,128]{1,0:T(8,128)(2,1)S(1)}, bf16[512,128]{1,0:T(8,128)(2,1)}, u32[]{:S(2)}) copy-start(bf16[512,128]{1,0:T(8,128)(2,1)} %constant.42.clone.refs_13_) | copy-start | bytes 393220
  8.1 0.9 %copy-start.7 = (bf16[256,256]{1,0:T(8,128)(2,1)S(1)}, bf16[256,256]{1,0:T(8,128)(2,1)}, u32[]{:S(2)}) copy-start(bf16[256,256]{1,0:T(8,128)(2,1)} %constant.41.clone.refs_12_) | copy-start | bytes 393220
  9.0 0.9 %copy-start.8 = (bf16[256,256]{1,0:T(8,128)(2,1)S(1)}, bf16[256,256]{1,0:T(8,128)(2,1)}, u32[]{:S(2)}) copy-start(bf16[256,256]{1,0:T(8,128)(2,1)} %constant.40.clone.refs_11_) | copy-start | bytes 393220
  9.9 0.9 %copy-start.9 = (f32[256,128]{1,0:T(8,128)S(1)}, f32[256,128]{1,0:T(8,128)}, u32[]{:S(2)}) copy-start(f32[256,128]{1,0:T(8,128)} %constant.33.clone.refs_4_) | copy-start | bytes 393220
  10.8 0.9 %copy-start.10 = (f32[256,128]{1,0:T(8,128)S(1)}, f32[256,128]{1,0:T(8,128)}, u32[]{:S(2)}) copy-start(f32[256,128]{1,0:T(8,128)} %constant.32.clone.refs_3_) | copy-start | bytes 393220
  11.7 0.9 %copy-start.11 = (bf16[256,256]{1,0:T(8,128)(2,1)S(1)}, bf16[256,256]{1,0:T(8,128)(2,1)}, u32[]{:S(2)}) copy-start(bf16[256,256]{1,0:T(8,128)(2,1)} %constant.31.clone.refs_2_) | copy-start | bytes 393220
  12.6 0.9 %copy-start.12 = (bf16[256,256]{1,0:T(8,128)(2,1)S(1)}, bf16[256,256]{1,0:T(8,128)(2,1)}, u32[]{:S(2)}) copy-start(bf16[256,256]{1,0:T(8,128)(2,1)} %constant.30.clone.refs_1_) | copy-start | bytes 393220
  13.5 0.8 %copy-start.13 = (bf16[256,32]{1,0:T(8,128)(2,1)S(1)}, bf16[256,32]{1,0:T(8,128)(2,1)}, u32[]{:S(2)}) copy-start(bf16[256,32]{1,0:T(8,128)(2,1)} %constant.36.clone.refs_7_) | copy-start | bytes 49156
  14.3 0.8 %copy-start.14 = (bf16[256,32]{1,0:T(8,128)(2,1)S(1)}, bf16[256,32]{1,0:T(8,128)(2,1)}, u32[]{:S(2)}) copy-start(bf16[256,32]{1,0:T(8,128)(2,1)} %constant.35.clone.refs_6_) | copy-start | bytes 49156

commit v3 on v2

--- a/solution.py
+++ b/solution.py
@@ -568,7 +568,7 @@
                 pltpu.SemaphoreType.DMA((8, SIDE)),
             ],
             compiler_params=pltpu.CompilerParams(
-                collective_id=0, has_side_effects=True, vmem_limit_bytes=48 * 1024 * 1024
+                collective_id=0, has_side_effects=True, vmem_limit_bytes=67043328
             ),
         )(flat, *[jnp.asarray(table) for table in tables])
         return potential.reshape(cells_a, cells_b, length), energies[0, :2]

time: 79.3 us -> 64.8 us (0.82)
  local copies, waits for them, and re-layouts: 15.7 us -> 2.87 us
  Pallas kernels: 62.3 us -> 61.2 us
    unnamed x33 -> x1, local copies, waits for them, and re-layouts: 15.2 us -> 1.67 us
    pallas_call x1, Pallas kernels: 62.3 us -> 61.2 us  [shards(): pl.pallas_call(kernel, out_shape=(jax.ShapeDtypeStruct((256, 256), F32),...]
where the time goes in v3:
time: 64.8 us; the launch traced here: 64.7 us
  Pallas kernels  61.2 us (94%)
  local copies, waits for them, and re-layouts  2.87 us (4%)
    pallas_call x1, Pallas kernels, shards(): pl.pallas_call(kernel, out_shape=(jax.ShapeDtypeStruct((256, 256), F32),...  61.2 us
    unnamed x1, local copies, waits for them, and re-layouts  1.67 us

profile of v3, /device:TPU:1, one launch (start us, length us, event | category | flops | bytes accessed | tf_op | source)
XLA Modules:
  0.0 64.7 jit_solution(13126433561051848482)
XLA Ops:
  0.6 61.2 %shard_map.167 = (f32[256,256]{1,0:T(8,128)}, f32[8,128]{1,0:T(8,128)}) custom-call(f32[256,256]{1,0:T(8,128)} %bitcast.4, bf16[256,256]{1,0:T(8,128)(2,1)} %constant.30.clone.refs_1_, bf16[256,256]{1,0:T(8,128)(2,1)} %constant.31.clone.refs_2_, f32[256,128]{1,0:T(8,128)} %constant.32.clone.refs_3_, f32[256,128]{1,0:T(8,128)} %constant.33.clone.refs_4_, ...), custom_call_target="tpu_custom_call" | custom-call | tf_op jit(solution)/shard_map/pallas_call | solution.py:542
  61.8 1.2 %slice_bitcast_fusion = f32[2]{0:T(128)} fusion(f32[8,128]{1,0:T(8,128)} %get-tuple-element.5), kind=kLoop, calls=%fused_computation | loop fusion | bytes 16 | tf_op jit(solution)/shard_map/squeeze | solution.py:574
  63.0 1.7 %copy.19 = f32[16,16,256]{2,1,0:T(8,128)} copy(f32[16,16,256]{2,1,0:T(8,128)} %bitcast.5) | data formatting | bytes 524288

commit v4 on v3

--- a/solution.py
+++ b/solution.py
@@ -152,6 +152,7 @@
 
 MESH = pl.DeviceIdType.MESH
 SIDE = 16
+WIDE = 24
 HALF = 128
 F32 = jnp.float32
 BF16 = jnp.bfloat16
@@ -192,19 +193,29 @@
                 store(8 * h + i, a, rows[i][part * SIDE : (part + 1) * SIDE])
 
 
-def local_entries(field, expand_x, expand_y, expand_z, energy):
-    pieces = split(field)
+def green_rows(sines, basis_rows):
+    return jnp.concatenate([sines[x : x + 1, :] * basis_rows for x in range(SIDE)], axis=0)
+
+
+def weighted_rows(table, values):
+    total = table[:WIDE] * values[0:1, :]
+    for x in range(1, SIDE):
+        total += table[x * WIDE : (x + 1) * WIDE] * values[x : x + 1, :]
+    return total
+
+
+def local_entries(folded, expand_y, expand_z, select_x):
+    pieces = split(folded)
     outcome = []
     for tile in range(4):
         lanes = slice(tile * 256, (tile + 1) * 256)
-        mixed = dot3(pieces, (expand_x[0][:, lanes], expand_x[1][:, lanes]))
-        total = mixed[:SIDE] * expand_z[0:1, lanes]
+        mixed = dot3(pieces, (expand_y[0][:, lanes], expand_y[1][:, lanes]))
+        total = mixed[:WIDE] * expand_z[0:1, lanes]
         for k in range(1, SIDE):
-            total += mixed[k * SIDE : (k + 1) * SIDE] * expand_z[k : k + 1, lanes]
-        summed = jnp.sum(total * expand_y[:, lanes], axis=0, keepdims=True)
+            total += mixed[k * WIDE : (k + 1) * WIDE] * expand_z[k : k + 1, lanes]
+        chosen = select_x[0:32, lanes].astype(F32)[:WIDE]
+        summed = jnp.sum(total * chosen, axis=0, keepdims=True)
         outcome += [summed[:, :HALF], summed[:, HALF:]]
-    lane = lax.broadcasted_iota(jnp.int32, (1, HALF), 1)
-    outcome[7] = jnp.where(lane == HALF - 1, energy, outcome[7])
     return outcome
 
 
@@ -322,7 +333,7 @@
     return total
 
 
-CONSTANTS = 15
+CONSTANTS = 16
 
 
 def kernel(*refs):
@@ -335,12 +346,12 @@
     sends = scratch[1 + CONSTANTS : 5 + CONSTANTS]
     lands = scratch[5 + CONSTANTS : 9 + CONSTANTS]
     (
-        mats, spectrum, field_ref, inverse_ref, expand_high, expand_low, expand_y, expand_z,
+        mats, spectrum, field_ref, inverse_ref, expand_high, expand_low, expand_z, pair_sum, half_rows, green, folded,
         onehot, small_send, small_land, local_sem, send_sem, recv_sem,
     ) = scratch[9 + CONSTANTS :]
     (
         sine_high, sine_low, eigen_wide, edge_wide, lane_rows, basis_high, basis_low, select,
-        gather, spread, column_high, column_low, heads, root, power,
+        gather, spread, column_high, column_low, heads, root, power, basis_rows,
     ) = held
     p = lax.axis_index("gx")
     q = lax.axis_index("gy")
@@ -415,19 +426,29 @@
         copy.wait()
     for tile in range(4):
         lanes = slice(tile * 256, (tile + 1) * 256)
-        expand_high[:, lanes] = dot(basis_high[...], select[0:32, lanes]).astype(BF16)
-        expand_low[:, lanes] = dot(basis_low[...], select[0:32, lanes]).astype(BF16)
-        expand_y[:, lanes] = dot(basis_high[at(p), :], select[32:64, lanes]) + dot(
-            basis_low[at(p), :], select[32:64, lanes]
-        )
+        expand_high[:, lanes] = dot(basis_high[...], select[32:64, lanes]).astype(BF16)
+        expand_low[:, lanes] = dot(basis_low[...], select[32:64, lanes]).astype(BF16)
         expand_z[:, lanes] = dot(basis_high[at(q), :], select[64:96, lanes]) + dot(
             basis_low[at(q), :], select[64:96, lanes]
         )
+    cube = ((N + 1) / 2.0) ** 3
+    pair_sum[:, :HALF] = eigen_wide[...] + lane_rows[0:1, :HALF]
+    pair_sum[:, HALF:] = eigen_wide[...] + lane_rows[0:1, HALF:]
+    near = sine_high[at(p), :].astype(F32) + sine_low[at(p), :].astype(F32)
+    lead_high, lead_low = split(green_rows(near, basis_rows[...]))
+
+    def fill(k, carry):
+        shift = eigen_wide[pl.ds(q * SIDE + k, 1), :]
+        shift = jnp.concatenate([shift, shift], axis=1)
+        weights = split(1.0 / ((pair_sum[...] + shift) * cube))
+        green[k] = dot3((lead_high, lead_low), weights)
+        return carry
+
+    lax.fori_loop(0, SIDE, fill, 0)
     eigen_y = eigen_wide[at(p), :]
     eigen_y = jnp.concatenate([eigen_y, eigen_y], axis=1) + lane_rows[0:1, :]
     eigen_z = eigen_wide[at(q), :]
     eigen_z = jnp.concatenate([eigen_z, eigen_z], axis=1)
-    cube = ((N + 1) / 2.0) ** 3
     for k in range(SIDE):
         rows = slice(k * SIDE, (k + 1) * SIDE)
         inverse_ref[rows, :] = 1.0 / ((eigen_y + eigen_z[k : k + 1, :]) * cube)
@@ -435,20 +456,26 @@
 
     collect(0, "gy", q, True)
     launch(1, mat(), "gx", p)
+    half_rows[...] = dot3(split(mat()), sines())
+
+    def fold(k, carry):
+        folded[pl.ds(pl.multiple_of(k * WIDE, 8), WIDE), :] = weighted_rows(
+            green[k], half_rows[at(k), :]
+        )
+        return carry
+
+    lax.fori_loop(0, SIDE, fold, 0)
+    entries = local_entries(folded[...], (expand_high, expand_low), expand_z, select)
+    small(4, 0, jnp.concatenate(entries, axis=0), "gy", q)
+    small(5, 1, small_total(4, 0, "gy", q), "gx", p)
+
     collect(1, "gx", p, False)
-
     value = dot3(split(mat()), sines())
     spectrum[...] = value
     field = value * inverse_ref[...]
     field_ref[...] = field
     energy = jnp.sum(jnp.sum(value * field, axis=1, keepdims=True), axis=0, keepdims=True)
-    entries = local_entries(
-        field, (expand_high, expand_low), expand_y, expand_z, energy
-    )
-    small(4, 0, jnp.concatenate(entries, axis=0), "gx", p)
-    partial = small_total(4, 0, "gx", p)
-    small(5, 1, partial, "gy", q)
-    entries = small_total(5, 1, "gy", q)
+    entries = small_total(5, 1, "gx", p)
 
     at_y = (sine_high[at(p), :], sine_low[at(p), :])
     at_z = (sine_high[at(q), :], sine_low[at(q), :])
@@ -470,22 +497,20 @@
         mats[1][rows, :] = total[:, HALF:]
     launch(2, mat(), "gx", p)
     second = jnp.sum(jnp.sum(second, axis=1, keepdims=True), axis=0, keepdims=True)
-    small(6, 2, jnp.broadcast_to(second, (8, HALF)), "gx", p)
+    lane = lax.broadcasted_iota(jnp.int32, (8, HALF), 1)
+    small(6, 2, jnp.where(lane == 0, energy, second), "gx", p)
     collect(2, "gx", p, True)
     launch(3, mat(), "gy", q)
     small(7, 3, small_total(6, 2, "gx", p), "gy", q)
     collect(3, "gy", q, False)
     out_ref[...] = dot3(split(mat()), sines())
-    second = small_total(7, 3, "gy", q)
-    lane = lax.broadcasted_iota(jnp.int32, (8, HALF), 1)
-    first = jnp.broadcast_to(entries[7:8, HALF - 1 :], (8, HALF))
-    energy_ref[...] = jnp.where(lane == 0, first, second) * (1.0 / (N + 1)) ** 3
+    energy_ref[...] = small_total(7, 3, "gy", q) * (1.0 / (N + 1)) ** 3
 
     axes = (("gy", q), ("gx", p), ("gx", p), ("gy", q))
     for phase in range(4):
         axis, me = axes[phase]
         finish_all(phase, sends[phase], lands[phase], axis, me, send_sem, recv_sem, SIDE, True)
-    axes = (("gx", p), ("gy", q), ("gx", p), ("gy", q))
+    axes = (("gy", q), ("gx", p), ("gx", p), ("gy", q))
     for index in range(4):
         axis, me = axes[index]
         finish_all(
@@ -528,6 +553,7 @@
         np.concatenate(heads, axis=0),
         root.astype(plain),
         power.astype(plain),
+        np.ascontiguousarray(basis.T[:WIDE]).astype(plain),
     ]
 
 
@@ -559,7 +585,10 @@
                 pltpu.VMEM((256, LANES), BF16),
                 pltpu.VMEM((256, LANES), BF16),
                 pltpu.VMEM((SIDE, LANES), F32),
-                pltpu.VMEM((SIDE, LANES), F32),
+                grid,
+                grid,
+                pltpu.VMEM((SIDE, SIDE * WIDE, 256), F32),
+                pltpu.VMEM((SIDE * WIDE, 256), F32),
                 pltpu.VMEM((LANES, 256), BF16),
                 [pltpu.VMEM((8, HALF), F32)] * 4,
                 [pltpu.VMEM((8 * SIDE, HALF), F32)] * 4,

time: 64.8 us -> 57.7 us (0.89)
  Pallas kernels: 61.2 us -> 54 us
    pallas_call x1, Pallas kernels: 61.2 us -> 54 us  [shards(): pl.pallas_call(kernel, out_shape=(jax.ShapeDtypeStruct((256, 256), F32),...]
where the time goes in v4:
time: 57.7 us; the launch traced here: 57.5 us
  Pallas kernels  54 us (94%)
  local copies, waits for them, and re-layouts  2.87 us (5%)
  between operations  0.64 us (1%)
    pallas_call x1, Pallas kernels, shards(): pl.pallas_call(kernel, out_shape=(jax.ShapeDtypeStruct((256, 256), F32),...  54 us
    unnamed x1, local copies, waits for them, and re-layouts  1.67 us
    squeeze x1, local copies, waits for them, and re-layouts, shards(): return (potential.reshape(cells_a, cells_b, length), energies[0, :2])  1.2 us

profile of v4, /device:TPU:1, one launch (start us, length us, event | category | flops | bytes accessed | tf_op | source)
XLA Modules:
  0.0 57.5 jit_solution(15467915223480123133)
XLA Ops:
  0.6 54.0 %shard_map.176 = (f32[256,256]{1,0:T(8,128)}, f32[8,128]{1,0:T(8,128)}) custom-call(f32[256,256]{1,0:T(8,128)} %bitcast.4, bf16[256,256]{1,0:T(8,128)(2,1)} %constant.32.clone.refs_1_, bf16[256,256]{1,0:T(8,128)(2,1)} %constant.33.clone.refs_2_, f32[256,128]{1,0:T(8,128)} %constant.34.clone.refs_3_, f32[256,128]{1,0:T(8,128)} %constant.35.clone.refs_4_, ...), custom_call_target="tpu_custom_call" | custom-call | tf_op jit(solution)/shard_map/pallas_call | solution.py:568
  54.6 1.2 %slice_bitcast_fusion = f32[2]{0:T(128)} fusion(f32[8,128]{1,0:T(8,128)} %get-tuple-element.5), kind=kLoop, calls=%fused_computation | loop fusion | bytes 16 | tf_op jit(solution)/shard_map/squeeze | solution.py:603
  55.8 1.7 %copy.20 = f32[16,16,256]{2,1,0:T(8,128)} copy(f32[16,16,256]{2,1,0:T(8,128)} %bitcast.5) | data formatting | bytes 524288

commit v5 on v4

--- a/solution.py
+++ b/solution.py
@@ -194,7 +194,8 @@
 
 
 def green_rows(sines, basis_rows):
-    return jnp.concatenate([sines[x : x + 1, :] * basis_rows for x in range(SIDE)], axis=0)
+    rows = [sines[x : x + 1, :] * basis_rows for x in range(SIDE)]
+    return jnp.concatenate(rows + [sines * basis_rows[17:18], sines * basis_rows[18:19]], axis=0)
 
 
 def weighted_rows(table, values):
@@ -226,7 +227,7 @@
     return jnp.where(owner == lane // 32, 1.0, 0.0).astype(BF16)
 
 
-def surface_hats(entries, gather, spread, onehot, columns, heads, root, power, at_y, at_z, sines):
+def surface_planes(entries, gather, spread, onehot, columns, heads, root, power):
     product = jnp.concatenate(
         [gather[:, r * HALF : (r + 1) * HALF] * entries[r : r + 1, :] for r in range(8)], axis=1
     )
@@ -253,10 +254,8 @@
                     base = (px * 4 + py * 2 + pz) * 32 + face * 9
                     blocks.append(jnp.where((lane >= base) & (lane < base + 9), shape, 0.0))
     right = dot3(split(jnp.concatenate(blocks, axis=0)), columns)
-    hats = []
+    planes = []
     for face in range(3):
-        left = at_z if face == 1 else at_y
-        both = jnp.concatenate(left, axis=0)
         for normal in range(2):
             parts = []
             for odd in range(2):
@@ -264,28 +263,37 @@
                 high, low = split(right[start : start + 32])
                 stack = jnp.concatenate([high, low, high, low], axis=0)
                 parts.append(dot(heads[odd * 256 : (odd + 1) * 256, :], stack))
-            plane = split(power * (root * parts[0] + parts[1]))
-            first = dot(both, plane[0])
-            hats.append(first[:SIDE] + (first[SIDE:] + dot(left[0], plane[1])))
-    full = dot3(split(jnp.concatenate(hats[:4], axis=0)), sines)
-    last = dot3(split(jnp.concatenate(hats[4:], axis=0)), at_z, NT)
-    return full, last
-
-
-def source_block(k, full, last, edge_y, edge_z, edge_lane):
+            planes.append(split(power * (root * parts[0] + parts[1])))
+    return planes
+
+
+def few_rows(rows, matrix, dims=NN):
+    both = dot(jnp.concatenate(rows, axis=0), matrix[0], dims)
+    return both[:SIDE] + (both[SIDE:] + dot(rows[0], matrix[1], dims))
+
+
+def side_hats(planes, at_y, at_z, sines):
+    hat_y = dot3(
+        split(jnp.concatenate([few_rows(at_z, planes[2 + n]) for n in range(2)], axis=0)), sines
+    )
+    half = [few_rows(at_z, planes[4 + n], NT) for n in range(2)]
+    hat_x = dot3(split(jnp.concatenate(half, axis=0)), sines)
+    return hat_y, hat_x, [dot3(at_y, split(half[n]), NT) for n in range(2)]
+
+
+def corrected(k, shape, scale, hat_y, hat_x, edge, inverse, edge_green, at_x):
+    even = lax.broadcasted_iota(jnp.int32, (256, 256), 0) % 2 == 0
+    mixed = shape * scale + jnp.where(even, hat_y[0], hat_y[1]) * edge
+    value = few_rows(at_x, split(mixed * inverse), NT)
+    return value + hat_x[0] * edge_green[:SIDE] + hat_x[1] * edge_green[SIDE:]
+
+
+def source_block(k, hat_z, hat_y, last, edge_y, edge_z, edge_lane):
     ky = lax.broadcasted_iota(jnp.int32, (SIDE, 256), 0)
-    wide = jnp.concatenate([edge_y, edge_y], axis=1)
-    scale = edge_z[k : k + 1, :]
-    scale = jnp.concatenate([scale, scale], axis=1)
-    normal = k % 2
-    value = full[normal * SIDE : (normal + 1) * SIDE] * scale
-    side = jnp.where(
-        ky % 2 == 0,
-        full[2 * SIDE + k : 2 * SIDE + k + 1, :],
-        full[3 * SIDE + k : 3 * SIDE + k + 1, :],
-    )
-    value += side * wide
-    value += last[:SIDE, k : k + 1] * edge_lane[0] + last[SIDE:, k : k + 1] * edge_lane[1]
+    value = hat_z[k % 2] * edge_z[k : k + 1, :]
+    side = jnp.where(ky % 2 == 0, hat_y[k : k + 1, :], hat_y[SIDE + k : SIDE + k + 1, :])
+    value += side * edge_y
+    value += last[0][:, k : k + 1] * edge_lane[0] + last[1][:, k : k + 1] * edge_lane[1]
     return value
 
 
@@ -346,7 +354,7 @@
     sends = scratch[1 + CONSTANTS : 5 + CONSTANTS]
     lands = scratch[5 + CONSTANTS : 9 + CONSTANTS]
     (
-        mats, spectrum, field_ref, inverse_ref, expand_high, expand_low, expand_z, pair_sum, half_rows, green, folded,
+        mats, field_ref, inverse, shape_z, expand_high, expand_low, expand_z, pair_sum, half_rows, green, folded, hats, extra,
         onehot, small_send, small_land, local_sem, send_sem, recv_sem,
     ) = scratch[9 + CONSTANTS :]
     (
@@ -388,7 +396,7 @@
         start_all(phase, sends[phase], lands[phase], axis, me, send_sem, recv_sem, SIDE)
         lands[phase][at(me), :] = sends[phase][at(me), :]
 
-    def collect(phase, axis, me, strided):
+    def collect(phase, axis, me, strided, added=None):
         finish_all(phase, sends[phase], lands[phase], axis, me, send_sem, recv_sem, SIDE, False)
         land = lands[phase]
 
@@ -396,6 +404,8 @@
             return land[a * SIDE : (a + 1) * SIDE, h * HALF : (h + 1) * HALF]
 
         def store(g, h, piece):
+            if added is not None:
+                piece += added[g * SIDE : (g + 1) * SIDE, h * HALF : (h + 1) * HALF]
             if strided:
                 mats[h][pl.ds(g, SIDE, stride=SIDE), :] = piece
             else:
@@ -440,18 +450,12 @@
     def fill(k, carry):
         shift = eigen_wide[pl.ds(q * SIDE + k, 1), :]
         shift = jnp.concatenate([shift, shift], axis=1)
-        weights = split(1.0 / ((pair_sum[...] + shift) * cube))
-        green[k] = dot3((lead_high, lead_low), weights)
+        whole = 1.0 / ((pair_sum[...] + shift) * cube)
+        inverse[k] = whole
+        green[k] = dot3((lead_high, lead_low), split(whole))
         return carry
 
     lax.fori_loop(0, SIDE, fill, 0)
-    eigen_y = eigen_wide[at(p), :]
-    eigen_y = jnp.concatenate([eigen_y, eigen_y], axis=1) + lane_rows[0:1, :]
-    eigen_z = eigen_wide[at(q), :]
-    eigen_z = jnp.concatenate([eigen_z, eigen_z], axis=1)
-    for k in range(SIDE):
-        rows = slice(k * SIDE, (k + 1) * SIDE)
-        inverse_ref[rows, :] = 1.0 / ((eigen_y + eigen_z[k : k + 1, :]) * cube)
     onehot[...] = owner_map()
 
     collect(0, "gy", q, True)
@@ -471,35 +475,58 @@
 
     collect(1, "gx", p, False)
     value = dot3(split(mat()), sines())
-    spectrum[...] = value
-    field = value * inverse_ref[...]
+    field = value * jnp.concatenate([inverse[k, at(p), :] for k in range(SIDE)], axis=0)
     field_ref[...] = field
+    launch(2, field, "gx", p)
     energy = jnp.sum(jnp.sum(value * field, axis=1, keepdims=True), axis=0, keepdims=True)
     entries = small_total(5, 1, "gx", p)
 
-    at_y = (sine_high[at(p), :], sine_low[at(p), :])
+    at_x = at_y = (sine_high[at(p), :], sine_low[at(p), :])
     at_z = (sine_high[at(q), :], sine_low[at(q), :])
-    full, last = surface_hats(
+    planes = surface_planes(
         entries, gather, spread, onehot[...], (column_high[...], column_low[...]), heads,
-        root[...], power[...], at_y, at_z, sines(),
+        root[...], power[...],
     )
+    for n in range(2):
+        shape_z[n] = dot3(split(dot3(sines(), planes[n])), sines())
+    hat_y, hat_x, last = side_hats(planes, at_y, at_z, sines())
+    hats[0] = hat_y
+    hats[1] = hat_x
+
     edge_y = edge_wide[at(p), :]
+    edge_y = jnp.concatenate([edge_y, edge_y], axis=1)
     edge_z = edge_wide[at(q), :]
+    edge_z = jnp.concatenate([edge_z, edge_z], axis=1)
     edge_lane = (lane_rows[1:2, :], lane_rows[2:3, :])
-    second = jnp.zeros((SIDE, 256), F32)
+    near_z = [shape_z[n, at(p), :] for n in range(2)]
+    cross = jnp.zeros((SIDE, 256), F32)
     for k in range(SIDE):
-        rows = slice(k * SIDE, (k + 1) * SIDE)
-        total = field_ref[rows, :] + inverse_ref[rows, :] * source_block(
-            k, full, last, edge_y, edge_z, edge_lane
-        )
-        second += spectrum[rows, :] * total
-        mats[0][rows, :] = total[:, :HALF]
-        mats[1][rows, :] = total[:, HALF:]
-    launch(2, mat(), "gx", p)
-    second = jnp.sum(jnp.sum(second, axis=1, keepdims=True), axis=0, keepdims=True)
+        cross += field_ref[k * SIDE : (k + 1) * SIDE, :] * source_block(
+            k, near_z, hat_y, last, edge_y, edge_z, edge_lane
+        )
+    second = energy + jnp.sum(jnp.sum(cross, axis=1, keepdims=True), axis=0, keepdims=True)
     lane = lax.broadcasted_iota(jnp.int32, (8, HALF), 1)
     small(6, 2, jnp.where(lane == 0, energy, second), "gx", p)
-    collect(2, "gx", p, True)
+
+    edge = jnp.concatenate([edge_wide[...], edge_wide[...]], axis=1)
+
+    def correct(k, carry):
+        scale = edge_wide[pl.ds(q * SIDE + k, 1), :]
+        extra[at(k), :] = corrected(
+            k,
+            shape_z[lax.rem(k, 2)],
+            jnp.concatenate([scale, scale], axis=1),
+            (hats[0, pl.ds(k, 1), :], hats[0, pl.ds(SIDE + k, 1), :]),
+            (hats[1, pl.ds(k, 1), :], hats[1, pl.ds(SIDE + k, 1), :]),
+            edge,
+            inverse[k],
+            green[k, SIDE * WIDE :, :],
+            at_x,
+        )
+        return carry
+
+    lax.fori_loop(0, SIDE, correct, 0)
+    collect(2, "gx", p, True, extra)
     launch(3, mat(), "gy", q)
     small(7, 3, small_total(6, 2, "gx", p), "gy", q)
     collect(3, "gy", q, False)
@@ -581,14 +608,18 @@
                 *hold,
                 *[grid] * 8,
                 [pltpu.VMEM((256, HALF), F32)] * 2,
-                *[grid] * 3,
+                grid,
+                pltpu.VMEM((SIDE, 256, 256), F32),
+                pltpu.VMEM((2, 256, 256), F32),
                 pltpu.VMEM((256, LANES), BF16),
                 pltpu.VMEM((256, LANES), BF16),
                 pltpu.VMEM((SIDE, LANES), F32),
                 grid,
                 grid,
-                pltpu.VMEM((SIDE, SIDE * WIDE, 256), F32),
+                pltpu.VMEM((SIDE, SIDE * WIDE + 2 * SIDE, 256), F32),
                 pltpu.VMEM((SIDE * WIDE, 256), F32),
+                pltpu.VMEM((2, 2 * SIDE, 256), F32),
+                grid,
                 pltpu.VMEM((LANES, 256), BF16),
                 [pltpu.VMEM((8, HALF), F32)] * 4,
                 [pltpu.VMEM((8 * SIDE, HALF), F32)] * 4,

time: 57.7 us -> 52.4 us (0.908)
  Pallas kernels: 54 us -> 48.8 us
    pallas_call x1, Pallas kernels: 54 us -> 48.8 us  [shards(): pl.pallas_call(kernel, out_shape=(jax.ShapeDtypeStruct((256, 256), F32),...]
where the time goes in v5:
time: 52.4 us; the launch traced here: 52.3 us
  Pallas kernels  48.8 us (93%)
  local copies, waits for them, and re-layouts  2.87 us (5%)
  between operations  0.64 us (1%)
    pallas_call x1, Pallas kernels, shards(): pl.pallas_call(kernel, out_shape=(jax.ShapeDtypeStruct((256, 256), F32),...  48.8 us
    unnamed x1, local copies, waits for them, and re-layouts  1.67 us
    squeeze x1, local copies, waits for them, and re-layouts, shards(): return (potential.reshape(cells_a, cells_b, length), energies[0, :2])  1.2 us

profile of v5, /device:TPU:1, one launch (start us, length us, event | category | flops | bytes accessed | tf_op | source)
XLA Modules:
  0.0 52.3 jit_solution(13932315241884047133)
XLA Ops:
  0.6 48.8 %shard_map.176 = (f32[256,256]{1,0:T(8,128)}, f32[8,128]{1,0:T(8,128)}) custom-call(f32[256,256]{1,0:T(8,128)} %bitcast.4, bf16[256,256]{1,0:T(8,128)(2,1)} %constant.32.clone.refs_1_, bf16[256,256]{1,0:T(8,128)(2,1)} %constant.33.clone.refs_2_, f32[256,128]{1,0:T(8,128)} %constant.34.clone.refs_3_, f32[256,128]{1,0:T(8,128)} %constant.35.clone.refs_4_, ...), custom_call_target="tpu_custom_call" | custom-call | tf_op jit(solution)/shard_map/pallas_call | solution.py:595
  49.4 1.2 %slice_bitcast_fusion = f32[2]{0:T(128)} fusion(f32[8,128]{1,0:T(8,128)} %get-tuple-element.5), kind=kLoop, calls=%fused_computation | loop fusion | bytes 16 | tf_op jit(solution)/shard_map/squeeze | solution.py:634
  50.6 1.7 %copy.20 = f32[16,16,256]{2,1,0:T(8,128)} copy(f32[16,16,256]{2,1,0:T(8,128)} %bitcast.5) | data formatting | bytes 524288

commit v6 on v5

--- a/solution.py
+++ b/solution.py
@@ -153,6 +153,8 @@
 MESH = pl.DeviceIdType.MESH
 SIDE = 16
 WIDE = 24
+EARLY = 2
+VMEM_LIMIT = 67043328 - 1024 * 1024
 HALF = 128
 F32 = jnp.float32
 BF16 = jnp.bfloat16
@@ -205,7 +207,7 @@
     return total
 
 
-def local_entries(folded, expand_y, expand_z, select_x):
+def local_entries(folded, expand_y, expand_z, select):
     pieces = split(folded)
     outcome = []
     for tile in range(4):
@@ -214,7 +216,7 @@
         total = mixed[:WIDE] * expand_z[0:1, lanes]
         for k in range(1, SIDE):
             total += mixed[k * WIDE : (k + 1) * WIDE] * expand_z[k : k + 1, lanes]
-        chosen = select_x[0:32, lanes].astype(F32)[:WIDE]
+        chosen = select[tile][0:32, :].astype(F32)[:WIDE]
         summed = jnp.sum(total * chosen, axis=0, keepdims=True)
         outcome += [summed[:, :HALF], summed[:, HALF:]]
     return outcome
@@ -229,16 +231,19 @@
 
 def surface_planes(entries, gather, spread, onehot, columns, heads, root, power):
     product = jnp.concatenate(
-        [gather[:, r * HALF : (r + 1) * HALF] * entries[r : r + 1, :] for r in range(8)], axis=1
+        [gather[r][...] * entries[r : r + 1, :] for r in range(8)], axis=1
     )
     high, rest = product.astype(BF16), None
     rest = product - high.astype(F32)
     middle = rest.astype(BF16)
     low = (rest - middle.astype(F32)).astype(BF16)
     moments = dot(high, onehot) + (dot(middle, onehot) + dot(low, onehot))
-    shape = moments[0:1, :] * spread[0]
+    shape = moments[0:1, :] * spread[0][0:8, :]
     for slot in range(1, 45):
-        shape += moments[slot : slot + 1, :] * spread[slot]
+        shape += moments[slot : slot + 1, :] * spread[0][slot * 8 : slot * 8 + 8, :]
+    ninth = jnp.sum(moments * spread[1][...], axis=0, keepdims=True)
+    below = lax.broadcasted_iota(jnp.int32, (8, 256), 0) == 0
+    shape = jnp.concatenate([shape, jnp.where(below, ninth, 0.0)], axis=0)
     lane = lax.broadcasted_iota(jnp.int32, (SIDE, 256), 1)
     blocks = []
     for face in range(3):
@@ -262,7 +267,7 @@
                 start = ((face * 2 + normal) * 2 + odd) * 32
                 high, low = split(right[start : start + 32])
                 stack = jnp.concatenate([high, low, high, low], axis=0)
-                parts.append(dot(heads[odd * 256 : (odd + 1) * 256, :], stack))
+                parts.append(dot(heads[odd][...], stack))
             planes.append(split(power * (root * parts[0] + parts[1])))
     return planes
 
@@ -273,36 +278,45 @@
 
 
 def side_hats(planes, at_y, at_z, sines):
-    hat_y = dot3(
-        split(jnp.concatenate([few_rows(at_z, planes[2 + n]) for n in range(2)], axis=0)), sines
-    )
+    half_y = split(jnp.concatenate([few_rows(at_z, planes[2 + n]) for n in range(2)], axis=0))
+    hat_y, turned = dot3(half_y, sines), dot3(sines, half_y, NT)
     half = [few_rows(at_z, planes[4 + n], NT) for n in range(2)]
     hat_x = dot3(split(jnp.concatenate(half, axis=0)), sines)
-    return hat_y, hat_x, [dot3(at_y, split(half[n]), NT) for n in range(2)]
-
-
-def corrected(k, shape, scale, hat_y, hat_x, edge, inverse, edge_green, at_x):
-    even = lax.broadcasted_iota(jnp.int32, (256, 256), 0) % 2 == 0
-    mixed = shape * scale + jnp.where(even, hat_y[0], hat_y[1]) * edge
-    value = few_rows(at_x, split(mixed * inverse), NT)
+    near_x = [dot3(at_y, split(half[n]), NT) for n in range(2)]
+    half_z = split(jnp.concatenate([few_rows(at_y, planes[n]) for n in range(2)], axis=0))
+    return hat_y, turned, hat_x, near_x, dot3(half_z, sines)
+
+
+def corrected(shape, scale, column, edge_lane, hat_x, inverse, edge_green, at_x):
+    even = lax.broadcasted_iota(jnp.int32, (1, 256), 1) % 2 == 0
+    mixed = shape * scale + jnp.where(even, column[0], column[1]) * edge_lane
+    value = few_rows(at_x, split(mixed * inverse))
     return value + hat_x[0] * edge_green[:SIDE] + hat_x[1] * edge_green[SIDE:]
 
 
 def source_block(k, hat_z, hat_y, last, edge_y, edge_z, edge_lane):
     ky = lax.broadcasted_iota(jnp.int32, (SIDE, 256), 0)
-    value = hat_z[k % 2] * edge_z[k : k + 1, :]
+    value = hat_z[(k % 2) * SIDE : (k % 2 + 1) * SIDE] * edge_z[k : k + 1, :]
     side = jnp.where(ky % 2 == 0, hat_y[k : k + 1, :], hat_y[SIDE + k : SIDE + k + 1, :])
     value += side * edge_y
     value += last[0][:, k : k + 1] * edge_lane[0] + last[1][:, k : k + 1] * edge_lane[1]
     return value
 
 
+def offset(axis, i):
+    if axis == "gy":
+        return 8 + (1 - 2 * (i % 2)) * ((i + 1) // 2)
+    j = i // 2
+    return 4 + (1 - 2 * (j % 2)) * ((j + 1) // 2) + 8 * (i % 2) + 8 * (i // 14)
+
+
 def start_all(phase, source, target, axis, me, send_sem, recv_sem, rows):
-    def body(d, carry):
+    def body(i, carry):
+        d = offset(axis, i)
         copy_of(phase, source, target, axis, me, send_sem, recv_sem, rows, d).start()
         return carry
 
-    lax.fori_loop(1, SIDE, body, 0)
+    lax.fori_loop(0, SIDE - 1, body, 0)
 
 
 def copy_of(phase, source, target, axis, me, send_sem, recv_sem, rows, d):
@@ -341,32 +355,54 @@
     return total
 
 
-CONSTANTS = 16
-
-
-def kernel(*refs):
-    charge_hbm = refs[0]
-    held_hbm = refs[1 : 1 + CONSTANTS]
-    out_ref, energy_ref = refs[1 + CONSTANTS : 3 + CONSTANTS]
-    scratch = refs[3 + CONSTANTS :]
-    charge = scratch[0]
-    held = scratch[1 : 1 + CONSTANTS]
-    sends = scratch[1 + CONSTANTS : 5 + CONSTANTS]
-    lands = scratch[5 + CONSTANTS : 9 + CONSTANTS]
+def unpack(plain, narrow, cut):
+    return dict(
+        eigen_wide=cut(plain, 0, 256, 0, 128),
+        edge_wide=cut(plain, 0, 256, 128, 256),
+        lane_rows=cut(plain, 256, 264, 0, 256),
+        basis_rows=cut(plain, 264, 288, 0, 256),
+        gather=[
+            cut(plain, 288 + SLOTS * (r // 2), 288 + SLOTS * (r // 2 + 1), r % 2 * 128, r % 2 * 128 + 128)
+            for r in range(8)
+        ],
+        spread=(cut(plain, 480, 864, 0, 256), cut(plain, 864, 912, 0, 256)),
+        root=cut(plain, 912, 1168, 0, 256),
+        sine_high=cut(narrow, 0, 256, 0, 256),
+        sine_low=cut(narrow, 256, 512, 0, 256),
+        basis_high=cut(narrow, 512, 768, 0, 128),
+        basis_low=cut(narrow, 512, 768, 128, 256),
+        select=[cut(narrow, 768 + 96 * t, 864 + 96 * t, 0, 256) for t in range(4)],
+        column_high=cut(narrow, 1152, 1408, 0, 256),
+        column_low=cut(narrow, 1408, 1664, 0, 256),
+        heads=[cut(narrow, 1664, 1920, 128 * odd, 128 * odd + 128) for odd in range(2)],
+    )
+
+
+def kernel(charge_hbm, plain_hbm, narrow_hbm, out_ref, energy_ref, *scratch):
+    charge, plain, narrow = scratch[:3]
+    sends = scratch[3:7]
+    lands = scratch[7:11]
     (
-        mats, field_ref, inverse, shape_z, expand_high, expand_low, expand_z, pair_sum, half_rows, green, folded, hats, extra,
-        onehot, small_send, small_land, local_sem, send_sem, recv_sem,
-    ) = scratch[9 + CONSTANTS :]
-    (
-        sine_high, sine_low, eigen_wide, edge_wide, lane_rows, basis_high, basis_low, select,
-        gather, spread, column_high, column_low, heads, root, power, basis_rows,
-    ) = held
+        mats, field_ref, inverse, shape_z, expand_high, expand_low, expand_z, pair_sum, half_rows,
+        green, folded, hats, extra, turned_y, power, own, onehot, small_send, small_land, local_sem,
+        send_sem, recv_sem,
+    ) = scratch[11:]
+    table = unpack(plain, narrow, lambda ref, a, b, c, d: ref.at[a:b, c:d])
+    eigen_wide, edge_wide, lane_rows = table["eigen_wide"], table["edge_wide"], table["lane_rows"]
+    sine_high, sine_low, select = table["sine_high"], table["sine_low"], table["select"]
     p = lax.axis_index("gx")
     q = lax.axis_index("gy")
 
-    copies = [pltpu.make_async_copy(charge_hbm, charge, local_sem.at[0])]
-    for i in range(CONSTANTS):
-        copies.append(pltpu.make_async_copy(held_hbm[i], held[i], local_sem.at[i + 1]))
+    pieces = (
+        (charge_hbm, charge),
+        (narrow_hbm.at[0:512, :], narrow.at[0:512, :]),
+        (narrow_hbm.at[512:1920, :], narrow.at[512:1920, :]),
+        (plain_hbm, plain),
+    )
+    copies = [
+        pltpu.make_async_copy(source, target, local_sem.at[i])
+        for i, (source, target) in enumerate(pieces)
+    ]
     for copy in copies:
         copy.start()
 
@@ -389,10 +425,10 @@
     def sines():
         return sine_high[...], sine_low[...]
 
-    def launch(phase, value, axis, me):
+    def launch(phase, value, axis, me, ready=None):
         sends[phase][...] = dot3(sines(), split(value), NT)
-        if phase == 0:
-            pl.semaphore_wait(barrier, 2 * (SIDE - 1))
+        if ready is not None:
+            ready()
         start_all(phase, sends[phase], lands[phase], axis, me, send_sem, recv_sem, SIDE)
         lands[phase][at(me), :] = sends[phase][at(me), :]
 
@@ -427,36 +463,50 @@
         )
         return sum_slots(small_land[index])
 
+    cube = ((N + 1) / 2.0) ** 3
+
+    def lead_rows():
+        near = sine_high[at(p), :].astype(F32) + sine_low[at(p), :].astype(F32)
+        return split(green_rows(near, table["basis_rows"][...]))
+
+    def fill(k, lead):
+        whole = 1.0 / ((pair_sum[...] + own[pl.ds(k, 1), :]) * cube)
+        inverse[k] = whole
+        green[k] = dot3(lead, split(whole))
+        return lead
+
+    def prepare():
+        copies[2].wait()
+        copies[3].wait()
+        for tile in range(4):
+            lanes = slice(tile * 256, (tile + 1) * 256)
+            chosen = select[tile]
+            basis = (table["basis_high"][...][:, :32], table["basis_low"][...][:, :32])
+            expand_high[:, lanes] = dot(basis[0], chosen[32:64, :]).astype(BF16)
+            expand_low[:, lanes] = dot(basis[1], chosen[32:64, :]).astype(BF16)
+            near = (table["basis_high"][at(q), :][:, :32], table["basis_low"][at(q), :][:, :32])
+            expand_z[:, lanes] = dot(near[0], chosen[64:96, :]) + dot(near[1], chosen[64:96, :])
+        for half in range(2):
+            lanes = slice(half * HALF, (half + 1) * HALF)
+            own[0:SIDE, lanes] = eigen_wide[at(q), :]
+            own[SIDE : 2 * SIDE, lanes] = edge_wide[at(q), :]
+        pair_sum[:, :HALF] = eigen_wide[...] + lane_rows[0:1, :HALF]
+        pair_sum[:, HALF:] = eigen_wide[...] + lane_rows[0:1, HALF:]
+        lax.fori_loop(0, EARLY, fill, lead_rows())
+        pl.semaphore_wait(barrier, 2 * (SIDE - 1))
+
+    def drain_big(phase, axis, me):
+        finish_all(phase, sends[phase], lands[phase], axis, me, send_sem, recv_sem, SIDE, True)
+
+    def drain_small(phase, index, axis, me):
+        finish_all(
+            phase, small_send[index], small_land[index], axis, me, send_sem, recv_sem, None, True
+        )
+
     copies[0].wait()
     copies[1].wait()
-    copies[2].wait()
-    launch(0, charge[...], "gy", q)
-
-    for copy in copies[3:]:
-        copy.wait()
-    for tile in range(4):
-        lanes = slice(tile * 256, (tile + 1) * 256)
-        expand_high[:, lanes] = dot(basis_high[...], select[32:64, lanes]).astype(BF16)
-        expand_low[:, lanes] = dot(basis_low[...], select[32:64, lanes]).astype(BF16)
-        expand_z[:, lanes] = dot(basis_high[at(q), :], select[64:96, lanes]) + dot(
-            basis_low[at(q), :], select[64:96, lanes]
-        )
-    cube = ((N + 1) / 2.0) ** 3
-    pair_sum[:, :HALF] = eigen_wide[...] + lane_rows[0:1, :HALF]
-    pair_sum[:, HALF:] = eigen_wide[...] + lane_rows[0:1, HALF:]
-    near = sine_high[at(p), :].astype(F32) + sine_low[at(p), :].astype(F32)
-    lead_high, lead_low = split(green_rows(near, basis_rows[...]))
-
-    def fill(k, carry):
-        shift = eigen_wide[pl.ds(q * SIDE + k, 1), :]
-        shift = jnp.concatenate([shift, shift], axis=1)
-        whole = 1.0 / ((pair_sum[...] + shift) * cube)
-        inverse[k] = whole
-        green[k] = dot3((lead_high, lead_low), split(whole))
-        return carry
-
-    lax.fori_loop(0, SIDE, fill, 0)
-    onehot[...] = owner_map()
+    launch(0, charge[...], "gy", q, prepare)
+    lax.fori_loop(EARLY, SIDE, fill, lead_rows())
 
     collect(0, "gy", q, True)
     launch(1, mat(), "gx", p)
@@ -471,6 +521,12 @@
     lax.fori_loop(0, SIDE, fold, 0)
     entries = local_entries(folded[...], (expand_high, expand_low), expand_z, select)
     small(4, 0, jnp.concatenate(entries, axis=0), "gy", q)
+    onehot[...] = owner_map()
+    root = table["root"][...]
+    square = root * root
+    fourth = square * square
+    power[...] = fourth * fourth * (fourth * (square * root))
+    drain_big(0, "gy", q)
     small(5, 1, small_total(4, 0, "gy", q), "gx", p)
 
     collect(1, "gx", p, False)
@@ -484,41 +540,37 @@
     at_x = at_y = (sine_high[at(p), :], sine_low[at(p), :])
     at_z = (sine_high[at(q), :], sine_low[at(q), :])
     planes = surface_planes(
-        entries, gather, spread, onehot[...], (column_high[...], column_low[...]), heads,
-        root[...], power[...],
+        entries, table["gather"], table["spread"], onehot[...],
+        (table["column_high"][...], table["column_low"][...]), table["heads"],
+        table["root"][...], power[...],
     )
-    for n in range(2):
-        shape_z[n] = dot3(split(dot3(sines(), planes[n])), sines())
-    hat_y, hat_x, last = side_hats(planes, at_y, at_z, sines())
-    hats[0] = hat_y
-    hats[1] = hat_x
-
+    hat_y, turned, hat_x, near_x, near_z = side_hats(planes, at_y, at_z, sines())
     edge_y = edge_wide[at(p), :]
     edge_y = jnp.concatenate([edge_y, edge_y], axis=1)
-    edge_z = edge_wide[at(q), :]
-    edge_z = jnp.concatenate([edge_z, edge_z], axis=1)
+    edge_z = own[SIDE : 2 * SIDE, :]
     edge_lane = (lane_rows[1:2, :], lane_rows[2:3, :])
-    near_z = [shape_z[n, at(p), :] for n in range(2)]
     cross = jnp.zeros((SIDE, 256), F32)
     for k in range(SIDE):
         cross += field_ref[k * SIDE : (k + 1) * SIDE, :] * source_block(
-            k, near_z, hat_y, last, edge_y, edge_z, edge_lane
+            k, near_z, hat_y, near_x, edge_y, edge_z, edge_lane
         )
     second = energy + jnp.sum(jnp.sum(cross, axis=1, keepdims=True), axis=0, keepdims=True)
     lane = lax.broadcasted_iota(jnp.int32, (8, HALF), 1)
     small(6, 2, jnp.where(lane == 0, energy, second), "gx", p)
 
-    edge = jnp.concatenate([edge_wide[...], edge_wide[...]], axis=1)
+    for n in range(2):
+        shape_z[n] = dot3(sines(), split(dot3(sines(), planes[n])), NT)
+    hats[...] = hat_x
+    turned_y[:, : 2 * SIDE] = turned
 
     def correct(k, carry):
-        scale = edge_wide[pl.ds(q * SIDE + k, 1), :]
+        rolled = pltpu.roll(turned_y[...], HALF - k, 1)
         extra[at(k), :] = corrected(
-            k,
             shape_z[lax.rem(k, 2)],
-            jnp.concatenate([scale, scale], axis=1),
-            (hats[0, pl.ds(k, 1), :], hats[0, pl.ds(SIDE + k, 1), :]),
-            (hats[1, pl.ds(k, 1), :], hats[1, pl.ds(SIDE + k, 1), :]),
-            edge,
+            own[pl.ds(SIDE + k, 1), :],
+            (rolled[:, 0:1], rolled[:, SIDE : SIDE + 1]),
+            lane_rows[3:4, :],
+            (hats[pl.ds(k, 1), :], hats[pl.ds(SIDE + k, 1), :]),
             inverse[k],
             green[k, SIDE * WIDE :, :],
             at_x,
@@ -528,21 +580,17 @@
     lax.fori_loop(0, SIDE, correct, 0)
     collect(2, "gx", p, True, extra)
     launch(3, mat(), "gy", q)
+    drain_big(1, "gx", p)
+    drain_big(2, "gx", p)
+    drain_small(4, 0, "gy", q)
+    drain_small(5, 1, "gx", p)
     small(7, 3, small_total(6, 2, "gx", p), "gy", q)
+    drain_small(6, 2, "gx", p)
     collect(3, "gy", q, False)
     out_ref[...] = dot3(split(mat()), sines())
+    drain_big(3, "gy", q)
     energy_ref[...] = small_total(7, 3, "gy", q) * (1.0 / (N + 1)) ** 3
-
-    axes = (("gy", q), ("gx", p), ("gx", p), ("gy", q))
-    for phase in range(4):
-        axis, me = axes[phase]
-        finish_all(phase, sends[phase], lands[phase], axis, me, send_sem, recv_sem, SIDE, True)
-    axes = (("gy", q), ("gx", p), ("gx", p), ("gy", q))
-    for index in range(4):
-        axis, me = axes[index]
-        finish_all(
-            4 + index, small_send[index], small_land[index], axis, me, send_sem, recv_sem, None, True
-        )
+    drain_small(7, 3, "gy", q)
 
 
 def constants():
@@ -558,6 +606,7 @@
     lane_rows[0] = eigen
     lane_rows[1] = sine_rows[0] * (parity == 0)
     lane_rows[2] = sine_rows[0] * (parity == 1)
+    lane_rows[3] = sine_rows[0]
     heads = []
     for odd in range(2):
         tables = [trig(parity_of, odd, np.arctan(2.0 * (np.arange(N) - (N - 1) / 2.0) / (N + 1))) for parity_of in range(2)]
@@ -566,22 +615,34 @@
             wide[:, 16 * k : 16 * k + table.shape[0]] = table.T
         high, low = pair(wide)
         heads.append(np.concatenate([high, high, low, low], axis=1))
-    plain = np.float32
-    return [
-        *pair(sine_rows),
-        np.repeat(eigen[:, None], HALF, 1).astype(plain),
-        np.repeat(sine_rows[0][:, None], HALF, 1).astype(plain),
-        lane_rows.astype(plain),
-        *pair(basis),
-        np.concatenate(list(select), axis=0).astype(jnp.bfloat16),
-        gather.astype(plain),
-        spread.astype(plain),
-        *pair(columns),
-        np.concatenate(heads, axis=0),
-        root.astype(plain),
-        power.astype(plain),
-        np.ascontiguousarray(basis.T[:WIDE]).astype(plain),
-    ]
+    plain = np.concatenate(
+        [
+            np.concatenate([np.repeat(v[:, None], HALF, 1) for v in (eigen, sine_rows[0])], axis=1),
+            lane_rows,
+            basis.T[:WIDE],
+            *[gather[:, 256 * t : 256 * (t + 1)] for t in range(4)],
+            spread[:, :8].reshape(8 * SLOTS, 256),
+            spread[:, 8],
+            root,
+        ],
+        axis=0,
+    ).astype(np.float32)
+    wide = np.zeros((N, HALF - 32))
+    high, low = pair(basis)
+    narrow = np.concatenate(
+        [
+            *pair(sine_rows),
+            np.concatenate([high, wide.astype(high.dtype), low, wide.astype(high.dtype)], axis=1),
+            *[
+                np.concatenate(list(select), axis=0)[:, 256 * t : 256 * (t + 1)].astype(jnp.bfloat16)
+                for t in range(4)
+            ],
+            *pair(columns),
+            np.concatenate(heads, axis=1),
+        ],
+        axis=0,
+    )
+    return plain, narrow
 
 
 def solution(mesh):
@@ -591,21 +652,20 @@
         cells_a, cells_b, length = charge_density.shape
         flat = charge_density.reshape(cells_a * cells_b, length)
         grid = pltpu.VMEM((256, 256), F32)
-        hold = [pltpu.VMEM(table.shape, table.dtype) for table in tables]
         potential, energies = pl.pallas_call(
             kernel,
             out_shape=(
-                jax.ShapeDtypeStruct((256, 256), F32),
-                jax.ShapeDtypeStruct((8, HALF), F32),
+                pltpu.VMEM((256, 256), F32),
+                pltpu.VMEM((8, HALF), F32),
             ),
-            in_specs=[pl.BlockSpec(memory_space=pl.ANY)] * (1 + CONSTANTS),
+            in_specs=[pl.BlockSpec(memory_space=pl.ANY)] * 3,
             out_specs=(
                 pl.BlockSpec(memory_space=pltpu.VMEM),
                 pl.BlockSpec(memory_space=pltpu.VMEM),
             ),
             scratch_shapes=[
                 grid,
-                *hold,
+                *[pltpu.VMEM(table.shape, table.dtype) for table in tables],
                 *[grid] * 8,
                 [pltpu.VMEM((256, HALF), F32)] * 2,
                 grid,
@@ -618,17 +678,20 @@
                 grid,
                 pltpu.VMEM((SIDE, SIDE * WIDE + 2 * SIDE, 256), F32),
                 pltpu.VMEM((SIDE * WIDE, 256), F32),
-                pltpu.VMEM((2, 2 * SIDE, 256), F32),
+                pltpu.VMEM((2 * SIDE, 256), F32),
                 grid,
+                pltpu.VMEM((256, HALF), F32),
+                grid,
+                pltpu.VMEM((2 * SIDE, 256), F32),
                 pltpu.VMEM((LANES, 256), BF16),
                 [pltpu.VMEM((8, HALF), F32)] * 4,
                 [pltpu.VMEM((8 * SIDE, HALF), F32)] * 4,
-                pltpu.SemaphoreType.DMA((1 + CONSTANTS,)),
+                pltpu.SemaphoreType.DMA((4,)),
                 pltpu.SemaphoreType.DMA((8, SIDE)),
                 pltpu.SemaphoreType.DMA((8, SIDE)),
             ],
             compiler_params=pltpu.CompilerParams(
-                collective_id=0, has_side_effects=True, vmem_limit_bytes=67043328
+                collective_id=0, has_side_effects=True, vmem_limit_bytes=VMEM_LIMIT
             ),
         )(flat, *[jnp.asarray(table) for table in tables])
         return potential.reshape(cells_a, cells_b, length), energies[0, :2]

time: 52.4 us -> 50.1 us (0.956)
  local copies, waits for them, and re-layouts: 2.87 us -> 1.22 us
  Pallas kernels: 48.8 us -> 48.1 us
    unnamed x1, local copies, waits for them, and re-layouts: 1.67 us -> 0.71 us
    squeeze x1, local copies, waits for them, and re-layouts: 1.2 us -> 0.51 us  [shards(): return (potential.reshape(cells_a, cells_b, length), energies[0, :2])]
    pallas_call x1, Pallas kernels: 48.8 us -> 48.1 us  [shards(): pl.pallas_call(kernel, out_shape=(pltpu.VMEM((256, 256), F32), pltpu.VMEM...]
where the time goes in v6:
time: 50.1 us; the launch traced here: 50 us
  Pallas kernels  48.1 us (96%)
  local copies, waits for them, and re-layouts  1.22 us (2%)
  between operations  0.64 us (1%)
    pallas_call x1, Pallas kernels, shards(): pl.pallas_call(kernel, out_shape=(pltpu.VMEM((256, 256), F32), pltpu.VMEM...  48.1 us

profile of v6, /device:TPU:1, one launch (start us, length us, event | category | flops | bytes accessed | tf_op | source)
XLA Modules:
  0.0 50.0 jit_solution(1110867767185143008)
XLA Ops:
  0.6 48.1 %shard_map.50 = (f32[256,256]{1,0:T(8,128)S(1)}, f32[8,128]{1,0:T(8,128)S(1)}) custom-call(f32[256,256]{1,0:T(8,128)} %bitcast.5, f32[1168,256]{1,0:T(8,128)} %constant.4.clone.plain_hbm, bf16[1920,256]{1,0:T(8,128)(2,1)} %constant.5.clone.narrow_hbm), custom_call_target="tpu_custom_call" | custom-call | tf_op jit(solution)/shard_map/pallas_call | solution.py:655
  48.7 0.7 %copy.6 = f32[16,16,256]{2,1,0:T(8,128)} copy(f32[16,16,256]{2,1,0:T(8,128)S(1)} %bitcast.4) | data formatting | bytes 524288
  49.5 0.5 %slice_bitcast_fusion = f32[2]{0:T(128)} fusion(f32[8,128]{1,0:T(8,128)S(1)} %get-tuple-element.5), kind=kLoop, calls=%fused_computation | loop fusion | bytes 16 | tf_op jit(solution)/shard_map/squeeze | solution.py:697

commit v7 on v6

--- a/solution.py
+++ b/solution.py
@@ -153,7 +153,8 @@
 MESH = pl.DeviceIdType.MESH
 SIDE = 16
 WIDE = 24
-EARLY = 2
+EARLY = 0
+UNROLL = 2
 VMEM_LIMIT = 67043328 - 1024 * 1024
 HALF = 128
 F32 = jnp.float32
@@ -279,18 +280,18 @@
 
 def side_hats(planes, at_y, at_z, sines):
     half_y = split(jnp.concatenate([few_rows(at_z, planes[2 + n]) for n in range(2)], axis=0))
-    hat_y, turned = dot3(half_y, sines), dot3(sines, half_y, NT)
+    hat_y = dot3(half_y, sines)
     half = [few_rows(at_z, planes[4 + n], NT) for n in range(2)]
     hat_x = dot3(split(jnp.concatenate(half, axis=0)), sines)
     near_x = [dot3(at_y, split(half[n]), NT) for n in range(2)]
     half_z = split(jnp.concatenate([few_rows(at_y, planes[n]) for n in range(2)], axis=0))
-    return hat_y, turned, hat_x, near_x, dot3(half_z, sines)
-
-
-def corrected(shape, scale, column, edge_lane, hat_x, inverse, edge_green, at_x):
-    even = lax.broadcasted_iota(jnp.int32, (1, 256), 1) % 2 == 0
-    mixed = shape * scale + jnp.where(even, column[0], column[1]) * edge_lane
-    value = few_rows(at_x, split(mixed * inverse))
+    return hat_y, hat_x, near_x, dot3(half_z, sines)
+
+
+def corrected(shape, scale, hat_y, edge, hat_x, inverse, edge_green, at_x):
+    even = lax.broadcasted_iota(jnp.int32, (256, 256), 0) % 2 == 0
+    mixed = shape * scale + jnp.where(even, hat_y[0], hat_y[1]) * edge
+    value = few_rows(at_x, split(mixed * inverse), NT)
     return value + hat_x[0] * edge_green[:SIDE] + hat_x[1] * edge_green[SIDE:]
 
 
@@ -303,49 +304,37 @@
     return value
 
 
-def offset(axis, i):
-    if axis == "gy":
-        return 8 + (1 - 2 * (i % 2)) * ((i + 1) // 2)
-    j = i // 2
-    return 4 + (1 - 2 * (j % 2)) * ((j + 1) // 2) + 8 * (i % 2) + 8 * (i // 14)
+FAR = {
+    "gx": (4, 12, 3, 11, 5, 13, 2, 10, 6, 14, 1, 9, 7, 15, 8),
+    "gy": (8, 7, 9, 6, 10, 5, 11, 4, 12, 3, 13, 2, 14, 1, 15),
+}
 
 
 def start_all(phase, source, target, axis, me, send_sem, recv_sem, rows):
-    def body(i, carry):
-        d = offset(axis, i)
-        copy_of(phase, source, target, axis, me, send_sem, recv_sem, rows, d).start()
-        return carry
-
-    lax.fori_loop(0, SIDE - 1, body, 0)
-
-
-def copy_of(phase, source, target, axis, me, send_sem, recv_sem, rows, d):
-    peer = lax.rem(me + d, SIDE)
-    if rows is None:
-        src = source
-    else:
-        src = source.at[pl.ds(pl.multiple_of(peer * rows, rows), rows), :]
-    count = source.shape[0] if rows is None else rows
+    for d in FAR[axis]:
+        peer = lax.rem(me + d, SIDE)
+        count = source.shape[0] if rows is None else rows
+        src = source if rows is None else source.at[pl.ds(pl.multiple_of(peer * rows, rows), rows), :]
+        pltpu.make_async_remote_copy(
+            src_ref=src,
+            dst_ref=target.at[pl.ds(pl.multiple_of(me * count, count), count), :],
+            send_sem=send_sem.at[phase],
+            recv_sem=recv_sem.at[phase],
+            device_id={axis: peer},
+            device_id_type=MESH,
+        ).start()
+
+
+def whole_of(phase, target, axis, me, send_sem, recv_sem):
+    rows = target.shape[0] // SIDE * (SIDE - 1)
     return pltpu.make_async_remote_copy(
-        src_ref=src,
-        dst_ref=target.at[pl.ds(pl.multiple_of(me * count, count), count), :],
-        send_sem=send_sem.at[phase, d],
-        recv_sem=recv_sem.at[phase, d],
-        device_id={axis: peer},
+        src_ref=target.at[0:rows, :],
+        dst_ref=target.at[0:rows, :],
+        send_sem=send_sem.at[phase],
+        recv_sem=recv_sem.at[phase],
+        device_id={axis: lax.rem(me + 1, SIDE)},
         device_id_type=MESH,
     )
-
-
-def finish_all(phase, source, target, axis, me, send_sem, recv_sem, rows, sent):
-    def body(d, carry):
-        copy = copy_of(phase, source, target, axis, me, send_sem, recv_sem, rows, d)
-        if sent:
-            copy.wait_send()
-        else:
-            copy.wait_recv()
-        return carry
-
-    lax.fori_loop(1, SIDE, body, 0)
 
 
 def sum_slots(ref):
@@ -384,7 +373,7 @@
     lands = scratch[7:11]
     (
         mats, field_ref, inverse, shape_z, expand_high, expand_low, expand_z, pair_sum, half_rows,
-        green, folded, hats, extra, turned_y, power, own, onehot, small_send, small_land, local_sem,
+        green, folded, hats, extra, power, own, onehot, small_send, small_land, local_sem,
         send_sem, recv_sem,
     ) = scratch[11:]
     table = unpack(plain, narrow, lambda ref, a, b, c, d: ref.at[a:b, c:d])
@@ -433,7 +422,7 @@
         lands[phase][at(me), :] = sends[phase][at(me), :]
 
     def collect(phase, axis, me, strided, added=None):
-        finish_all(phase, sends[phase], lands[phase], axis, me, send_sem, recv_sem, SIDE, False)
+        whole_of(phase, lands[phase], axis, me, send_sem, recv_sem).wait_recv()
         land = lands[phase]
 
         def load(a, h):
@@ -458,9 +447,7 @@
         small_land[index][pl.ds(pl.multiple_of(me * 8, 8), 8), :] = value
 
     def small_total(phase, index, axis, me):
-        finish_all(
-            phase, small_send[index], small_land[index], axis, me, send_sem, recv_sem, None, False
-        )
+        whole_of(phase, small_land[index], axis, me, send_sem, recv_sem).wait_recv()
         return sum_slots(small_land[index])
 
     cube = ((N + 1) / 2.0) ** 3
@@ -496,12 +483,10 @@
         pl.semaphore_wait(barrier, 2 * (SIDE - 1))
 
     def drain_big(phase, axis, me):
-        finish_all(phase, sends[phase], lands[phase], axis, me, send_sem, recv_sem, SIDE, True)
+        whole_of(phase, lands[phase], axis, me, send_sem, recv_sem).wait_send()
 
     def drain_small(phase, index, axis, me):
-        finish_all(
-            phase, small_send[index], small_land[index], axis, me, send_sem, recv_sem, None, True
-        )
+        whole_of(phase, small_land[index], axis, me, send_sem, recv_sem).wait_send()
 
     copies[0].wait()
     copies[1].wait()
@@ -544,7 +529,7 @@
         (table["column_high"][...], table["column_low"][...]), table["heads"],
         table["root"][...], power[...],
     )
-    hat_y, turned, hat_x, near_x, near_z = side_hats(planes, at_y, at_z, sines())
+    hat_y, hat_x, near_x, near_z = side_hats(planes, at_y, at_z, sines())
     edge_y = edge_wide[at(p), :]
     edge_y = jnp.concatenate([edge_y, edge_y], axis=1)
     edge_z = own[SIDE : 2 * SIDE, :]
@@ -559,25 +544,25 @@
     small(6, 2, jnp.where(lane == 0, energy, second), "gx", p)
 
     for n in range(2):
-        shape_z[n] = dot3(sines(), split(dot3(sines(), planes[n])), NT)
-    hats[...] = hat_x
-    turned_y[:, : 2 * SIDE] = turned
+        shape_z[n] = dot3(split(dot3(sines(), planes[n])), sines())
+    hats[0] = hat_y
+    hats[1] = hat_x
+    edge = jnp.concatenate([edge_wide[...], edge_wide[...]], axis=1)
 
     def correct(k, carry):
-        rolled = pltpu.roll(turned_y[...], HALF - k, 1)
         extra[at(k), :] = corrected(
             shape_z[lax.rem(k, 2)],
             own[pl.ds(SIDE + k, 1), :],
-            (rolled[:, 0:1], rolled[:, SIDE : SIDE + 1]),
-            lane_rows[3:4, :],
-            (hats[pl.ds(k, 1), :], hats[pl.ds(SIDE + k, 1), :]),
+            (hats[0, pl.ds(k, 1), :], hats[0, pl.ds(SIDE + k, 1), :]),
+            edge,
+            (hats[1, pl.ds(k, 1), :], hats[1, pl.ds(SIDE + k, 1), :]),
             inverse[k],
             green[k, SIDE * WIDE :, :],
             at_x,
         )
         return carry
 
-    lax.fori_loop(0, SIDE, correct, 0)
+    lax.fori_loop(0, SIDE, correct, 0, unroll=UNROLL)
     collect(2, "gx", p, True, extra)
     launch(3, mat(), "gy", q)
     drain_big(1, "gx", p)
@@ -678,17 +663,16 @@
                 grid,
                 pltpu.VMEM((SIDE, SIDE * WIDE + 2 * SIDE, 256), F32),
                 pltpu.VMEM((SIDE * WIDE, 256), F32),
-                pltpu.VMEM((2 * SIDE, 256), F32),
+                pltpu.VMEM((2, 2 * SIDE, 256), F32),
                 grid,
-                pltpu.VMEM((256, HALF), F32),
                 grid,
                 pltpu.VMEM((2 * SIDE, 256), F32),
                 pltpu.VMEM((LANES, 256), BF16),
                 [pltpu.VMEM((8, HALF), F32)] * 4,
                 [pltpu.VMEM((8 * SIDE, HALF), F32)] * 4,
                 pltpu.SemaphoreType.DMA((4,)),
-                pltpu.SemaphoreType.DMA((8, SIDE)),
-                pltpu.SemaphoreType.DMA((8, SIDE)),
+                pltpu.SemaphoreType.DMA((8,)),
+                pltpu.SemaphoreType.DMA((8,)),
             ],
             compiler_params=pltpu.CompilerParams(
                 collective_id=0, has_side_effects=True, vmem_limit_bytes=VMEM_LIMIT

time: 50.1 us -> 45 us (0.90)
  Pallas kernels: 48.1 us -> 43.1 us
    pallas_call x1, Pallas kernels: 48.1 us -> 43.1 us  [shards(): pl.pallas_call(kernel, out_shape=(pltpu.VMEM((256, 256), F32), pltpu.VMEM...]
where the time goes in v7:
time: 45 us; the launch traced here: 44.9 us
  Pallas kernels  43.1 us (96%)
  local copies, waits for them, and re-layouts  1.22 us (3%)
  between operations  0.64 us (1%)
    pallas_call x1, Pallas kernels, shards(): pl.pallas_call(kernel, out_shape=(pltpu.VMEM((256, 256), F32), pltpu.VMEM...  43.1 us

profile of v7, /device:TPU:1, one launch (start us, length us, event | category | flops | bytes accessed | tf_op | source)
XLA Modules:
  0.0 44.9 jit_solution(8434597955801672263)
XLA Ops:
  0.6 43.1 %shard_map.50 = (f32[256,256]{1,0:T(8,128)S(1)}, f32[8,128]{1,0:T(8,128)S(1)}) custom-call(f32[256,256]{1,0:T(8,128)} %bitcast.5, f32[1168,256]{1,0:T(8,128)} %constant.4.clone.plain_hbm, bf16[1920,256]{1,0:T(8,128)(2,1)} %constant.5.clone.narrow_hbm), custom_call_target="tpu_custom_call" | custom-call | tf_op jit(solution)/shard_map/pallas_call | solution.py:640
  43.7 0.7 %copy.6 = f32[16,16,256]{2,1,0:T(8,128)} copy(f32[16,16,256]{2,1,0:T(8,128)S(1)} %bitcast.4) | data formatting | bytes 524288
  44.4 0.5 %slice_bitcast_fusion = f32[2]{0:T(128)} fusion(f32[8,128]{1,0:T(8,128)S(1)} %get-tuple-element.5), kind=kLoop, calls=%fused_computation | loop fusion | bytes 16 | tf_op jit(solution)/shard_map/squeeze | solution.py:681

commit v8 on v7

--- a/solution.py
+++ b/solution.py
@@ -197,15 +197,20 @@
 
 
 def green_rows(sines, basis_rows):
-    rows = [sines[x : x + 1, :] * basis_rows for x in range(SIDE)]
-    return jnp.concatenate(rows + [sines * basis_rows[17:18], sines * basis_rows[18:19]], axis=0)
+    rows = [sines[x : x + 1, :] * basis_rows[:SIDE] for x in range(SIDE)]
+    rows += [sines * basis_rows[f : f + 1] for f in range(SIDE, SIDE + 3)]
+    return jnp.concatenate(rows, axis=0)
 
 
 def weighted_rows(table, values):
-    total = table[:WIDE] * values[0:1, :]
+    total = table[:SIDE] * values[0:1, :]
     for x in range(1, SIDE):
-        total += table[x * WIDE : (x + 1) * WIDE] * values[x : x + 1, :]
-    return total
+        total += table[x * SIDE : (x + 1) * SIDE] * values[x : x + 1, :]
+    rows = [total]
+    for f in range(SIDE, SIDE + 3):
+        rows.append(jnp.sum(table[f * SIDE : (f + 1) * SIDE] * values, axis=0, keepdims=True))
+    rows.append(jnp.zeros((WIDE - SIDE - 3, 256), F32))
+    return jnp.concatenate(rows, axis=0)
 
 
 def local_entries(folded, expand_y, expand_z, select):
@@ -238,7 +243,8 @@
     rest = product - high.astype(F32)
     middle = rest.astype(BF16)
     low = (rest - middle.astype(F32)).astype(BF16)
-    moments = dot(high, onehot) + (dot(middle, onehot) + dot(low, onehot))
+    moments = dot(jnp.concatenate([high, middle, low], axis=0), onehot)
+    moments = moments[:SLOTS] + (moments[SLOTS : 2 * SLOTS] + moments[2 * SLOTS :])
     shape = moments[0:1, :] * spread[0][0:8, :]
     for slot in range(1, 45):
         shape += moments[slot : slot + 1, :] * spread[0][slot * 8 : slot * 8 + 8, :]
@@ -397,16 +403,11 @@
 
     barrier = pltpu.get_barrier_semaphore()
 
-    def greet(d, carry):
-        pl.semaphore_signal(
-            barrier, inc=1, device_id={"gx": lax.rem(p + d, SIDE)}, device_id_type=MESH
-        )
-        pl.semaphore_signal(
-            barrier, inc=1, device_id={"gy": lax.rem(q + d, SIDE)}, device_id_type=MESH
-        )
-        return carry
-
-    lax.fori_loop(1, SIDE, greet, 0)
+    for axis, me in (("gx", p), ("gy", q)):
+        for d in FAR[axis]:
+            pl.semaphore_signal(
+                barrier, inc=1, device_id={axis: lax.rem(me + d, SIDE)}, device_id_type=MESH
+            )
 
     def at(index):
         return pl.ds(pl.multiple_of(index * SIDE, SIDE), SIDE)
@@ -557,7 +558,7 @@
             edge,
             (hats[1, pl.ds(k, 1), :], hats[1, pl.ds(SIDE + k, 1), :]),
             inverse[k],
-            green[k, SIDE * WIDE :, :],
+            green[k, 17 * SIDE :, :],
             at_x,
         )
         return carry
@@ -661,7 +662,7 @@
                 pltpu.VMEM((SIDE, LANES), F32),
                 grid,
                 grid,
-                pltpu.VMEM((SIDE, SIDE * WIDE + 2 * SIDE, 256), F32),
+                pltpu.VMEM((SIDE, 19 * SIDE, 256), F32),
                 pltpu.VMEM((SIDE * WIDE, 256), F32),
                 pltpu.VMEM((2, 2 * SIDE, 256), F32),
                 grid,

time: 45 us -> 44.5 us (0.989)
  Pallas kernels: 43.1 us -> 42.5 us
    pallas_call x1, Pallas kernels: 43.1 us -> 42.5 us  [shards(): pl.pallas_call(kernel, out_shape=(pltpu.VMEM((256, 256), F32), pltpu.VMEM...]
where the time goes in v8:
time: 44.5 us; the launch traced here: 44.4 us
  Pallas kernels  42.5 us (96%)
  local copies, waits for them, and re-layouts  1.22 us (3%)
  between operations  0.64 us (1%)
    pallas_call x1, Pallas kernels, shards(): pl.pallas_call(kernel, out_shape=(pltpu.VMEM((256, 256), F32), pltpu.VMEM...  42.5 us

profile of v8, /device:TPU:1, one launch (start us, length us, event | category | flops | bytes accessed | tf_op | source)
XLA Modules:
  0.0 44.4 jit_solution(7333640086682142722)
XLA Ops:
  0.6 42.5 %shard_map.50 = (f32[256,256]{1,0:T(8,128)S(1)}, f32[8,128]{1,0:T(8,128)S(1)}) custom-call(f32[256,256]{1,0:T(8,128)} %bitcast.5, f32[1168,256]{1,0:T(8,128)} %constant.4.clone.plain_hbm, bf16[1920,256]{1,0:T(8,128)(2,1)} %constant.5.clone.narrow_hbm), custom_call_target="tpu_custom_call" | custom-call | tf_op jit(solution)/shard_map/pallas_call | solution.py:641
  43.1 0.7 %copy.6 = f32[16,16,256]{2,1,0:T(8,128)} copy(f32[16,16,256]{2,1,0:T(8,128)S(1)} %bitcast.4) | data formatting | bytes 524288
  43.9 0.5 %slice_bitcast_fusion = f32[2]{0:T(128)} fusion(f32[8,128]{1,0:T(8,128)S(1)} %get-tuple-element.5), kind=kLoop, calls=%fused_computation | loop fusion | bytes 16 | tf_op jit(solution)/shard_map/squeeze | solution.py:682

commit v9 on v8

--- a/solution.py
+++ b/solution.py
@@ -12,8 +12,7 @@
 N = 256
 SLOTS = 48
 LANES = 1024
-SPARE = 7 * 128 + 112
-ENERGY_LANE = 1023
+SPARE = 128 + 112
 
 
 def harmonics(x, y, z):
@@ -119,7 +118,7 @@
                 values = ratio**l * table[which][l, m]
                 moments[slot] = project @ values @ project.T
             for i, j in entries:
-                if lane >= (group + 1) * 128 or (lane >= SPARE and group == 7):
+                if lane >= (group + 1) * 128 or (lane >= SPARE and group == 1):
                     position, spill = spill, spill + 1
                     assert group == 0
                 else:
@@ -146,7 +145,7 @@
             columns[base : base + tail.shape[0]] = tail
             head = trig(prow, odd, angle)
             rows[group, face, : head.shape[0]] = head
-    assert spill < ENERGY_LANE
+    assert spill <= 256
     root = 1.0 / np.sqrt(1.0 - np.outer(np.sin(angle) ** 2, np.sin(angle) ** 2))
     return sine_rows, eigen, basis, select, gather, spread, columns, rows, root, root**15
 
@@ -206,23 +205,25 @@
     total = table[:SIDE] * values[0:1, :]
     for x in range(1, SIDE):
         total += table[x * SIDE : (x + 1) * SIDE] * values[x : x + 1, :]
-    rows = [total]
-    for f in range(SIDE, SIDE + 3):
-        rows.append(jnp.sum(table[f * SIDE : (f + 1) * SIDE] * values, axis=0, keepdims=True))
-    rows.append(jnp.zeros((WIDE - SIDE - 3, 256), F32))
-    return jnp.concatenate(rows, axis=0)
+    other = [
+        jnp.sum(table[f * SIDE : (f + 1) * SIDE] * values, axis=0, keepdims=True)
+        for f in range(SIDE, SIDE + 3)
+    ]
+    even = jnp.concatenate([total[:8], *other[:2], jnp.zeros((6, 256), F32)], axis=0)
+    return even, jnp.concatenate([total[8:], other[2], jnp.zeros((7, 256), F32)], axis=0)
 
 
 def local_entries(folded, expand_y, expand_z, select):
-    pieces = split(folded)
+    pieces = [split(part) for part in folded]
     outcome = []
     for tile in range(4):
         lanes = slice(tile * 256, (tile + 1) * 256)
-        mixed = dot3(pieces, (expand_y[0][:, lanes], expand_y[1][:, lanes]))
-        total = mixed[:WIDE] * expand_z[0:1, lanes]
+        mixed = dot3(pieces[tile // 2], (expand_y[0][:, lanes], expand_y[1][:, lanes]))
+        total = mixed[:SIDE] * expand_z[0:1, lanes]
         for k in range(1, SIDE):
-            total += mixed[k * WIDE : (k + 1) * WIDE] * expand_z[k : k + 1, lanes]
-        chosen = select[tile][0:32, :].astype(F32)[:WIDE]
+            total += mixed[k * SIDE : (k + 1) * SIDE] * expand_z[k : k + 1, lanes]
+        start = SIDE * (tile // 2)
+        chosen = select[tile][start : start + SIDE, :].astype(F32)
         summed = jnp.sum(total * chosen, axis=0, keepdims=True)
         outcome += [summed[:, :HALF], summed[:, HALF:]]
     return outcome
@@ -231,7 +232,7 @@
 def owner_map():
     row = lax.broadcasted_iota(jnp.int32, (LANES, 256), 0)
     lane = lax.broadcasted_iota(jnp.int32, (LANES, 256), 1)
-    owner = jnp.where(row >= SPARE, 0, row // HALF)
+    owner = jnp.where((row >= SPARE) & (row < 256), 0, row // HALF)
     return jnp.where(owner == lane // 32, 1.0, 0.0).astype(BF16)
 
 
@@ -311,14 +312,27 @@
 
 
 FAR = {
-    "gx": (4, 12, 3, 11, 5, 13, 2, 10, 6, 14, 1, 9, 7, 15, 8),
-    "gy": (8, 7, 9, 6, 10, 5, 11, 4, 12, 3, 13, 2, 14, 1, 15),
+    "gx": (
+        (4, 1), (3, 1), (5, 1), (4, 0), (2, 1), (6, 1), (3, 0), (5, 0), (1, 1), (7, 1), (2, 0),
+        (6, 0), (0, 1), (1, 0), (7, 0),
+    ),
+    "gy": (
+        (2, 3), (2, 2), (1, 3), (3, 3), (1, 2), (3, 2), (2, 1), (2, 0), (1, 1), (3, 1), (1, 0),
+        (3, 0), (0, 3), (0, 2), (0, 1),
+    ),
 }
 
 
+def peer_of(axis, me, step):
+    if axis == "gx":
+        return lax.rem(me // 8 + step[1], 2) * 8 + lax.rem(me % 8 + step[0], 8)
+    cross = lax.rem(me % 4 // 2 + step[1] // 2, 2) * 2 + lax.rem(me % 2 + step[1] % 2, 2)
+    return lax.rem(me // 4 + step[0], 4) * 4 + cross
+
+
 def start_all(phase, source, target, axis, me, send_sem, recv_sem, rows):
-    for d in FAR[axis]:
-        peer = lax.rem(me + d, SIDE)
+    for step in FAR[axis]:
+        peer = peer_of(axis, me, step)
         count = source.shape[0] if rows is None else rows
         src = source if rows is None else source.at[pl.ds(pl.multiple_of(peer * rows, rows), rows), :]
         pltpu.make_async_remote_copy(
@@ -404,9 +418,9 @@
     barrier = pltpu.get_barrier_semaphore()
 
     for axis, me in (("gx", p), ("gy", q)):
-        for d in FAR[axis]:
+        for step in FAR[axis]:
             pl.semaphore_signal(
-                barrier, inc=1, device_id={axis: lax.rem(me + d, SIDE)}, device_id_type=MESH
+                barrier, inc=1, device_id={axis: peer_of(axis, me, step)}, device_id_type=MESH
             )
 
     def at(index):
@@ -499,13 +513,11 @@
     half_rows[...] = dot3(split(mat()), sines())
 
     def fold(k, carry):
-        folded[pl.ds(pl.multiple_of(k * WIDE, 8), WIDE), :] = weighted_rows(
-            green[k], half_rows[at(k), :]
-        )
+        folded[0, at(k), :], folded[1, at(k), :] = weighted_rows(green[k], half_rows[at(k), :])
         return carry
 
     lax.fori_loop(0, SIDE, fold, 0)
-    entries = local_entries(folded[...], (expand_high, expand_low), expand_z, select)
+    entries = local_entries((folded[0], folded[1]), (expand_high, expand_low), expand_z, select)
     small(4, 0, jnp.concatenate(entries, axis=0), "gy", q)
     onehot[...] = owner_map()
     root = table["root"][...]
@@ -605,7 +617,7 @@
         [
             np.concatenate([np.repeat(v[:, None], HALF, 1) for v in (eigen, sine_rows[0])], axis=1),
             lane_rows,
-            basis.T[:WIDE],
+            basis.T[[*range(0, 16, 2), *range(1, 16, 2), *range(16, WIDE)]],
             *[gather[:, 256 * t : 256 * (t + 1)] for t in range(4)],
             spread[:, :8].reshape(8 * SLOTS, 256),
             spread[:, 8],
@@ -614,6 +626,9 @@
         axis=0,
     ).astype(np.float32)
     wide = np.zeros((N, HALF - 32))
+    chosen = np.zeros_like(select[0])
+    chosen[[*range(10), *range(16, 25)]] = select[0][[*range(0, 17, 2), 17, *range(1, 16, 2), 18]]
+    select[0] = chosen
     high, low = pair(basis)
     narrow = np.concatenate(
         [
@@ -663,7 +678,7 @@
                 grid,
                 grid,
                 pltpu.VMEM((SIDE, 19 * SIDE, 256), F32),
-                pltpu.VMEM((SIDE * WIDE, 256), F32),
+                pltpu.VMEM((2, 256, 256), F32),
                 pltpu.VMEM((2, 2 * SIDE, 256), F32),
                 grid,
                 grid,

time: 44.5 us -> 43.2 us (0.971)
  Pallas kernels: 42.5 us -> 41.2 us
    pallas_call x1, Pallas kernels: 42.5 us -> 41.2 us  [shards(): pl.pallas_call(kernel, out_shape=(pltpu.VMEM((256, 256), F32), pltpu.VMEM...]
where the time goes in v9:
time: 43.2 us; the launch traced here: 43 us
  Pallas kernels  41.2 us (95%)
  local copies, waits for them, and re-layouts  1.22 us (3%)
  between operations  0.64 us (1%)
    pallas_call x1, Pallas kernels, shards(): pl.pallas_call(kernel, out_shape=(pltpu.VMEM((256, 256), F32), pltpu.VMEM...  41.2 us

profile of v9, /device:TPU:1, one launch (start us, length us, event | category | flops | bytes accessed | tf_op | source)
XLA Modules:
  0.0 43.0 jit_solution(4492338334182237187)
XLA Ops:
  0.6 41.2 %shard_map.50 = (f32[256,256]{1,0:T(8,128)S(1)}, f32[8,128]{1,0:T(8,128)S(1)}) custom-call(f32[256,256]{1,0:T(8,128)} %bitcast.5, f32[1168,256]{1,0:T(8,128)} %constant.4.clone.plain_hbm, bf16[1920,256]{1,0:T(8,128)(2,1)} %constant.5.clone.narrow_hbm), custom_call_target="tpu_custom_call" | custom-call | tf_op jit(solution)/shard_map/pallas_call | solution.py:656
  41.8 0.7 %copy.6 = f32[16,16,256]{2,1,0:T(8,128)} copy(f32[16,16,256]{2,1,0:T(8,128)S(1)} %bitcast.4) | data formatting | bytes 524288
  42.5 0.5 %slice_bitcast_fusion = f32[2]{0:T(128)} fusion(f32[8,128]{1,0:T(8,128)S(1)} %get-tuple-element.5), kind=kLoop, calls=%fused_computation | loop fusion | bytes 16 | tf_op jit(solution)/shard_map/squeeze | solution.py:697

commit v10 on v9

--- a/solution.py
+++ b/solution.py
@@ -152,7 +152,7 @@
 MESH = pl.DeviceIdType.MESH
 SIDE = 16
 WIDE = 24
-EARLY = 0
+EARLY = 1
 UNROLL = 2
 VMEM_LIMIT = 67043328 - 1024 * 1024
 HALF = 128

time: 43.2 us -> 42.8 us (level)
  no operation moved by 1% of the time
where the time goes in v10:
time: 42.8 us; the launch traced here: 42.6 us
  Pallas kernels  40.8 us (95%)
  local copies, waits for them, and re-layouts  1.22 us (3%)
  between operations  0.64 us (1%)
    pallas_call x1, Pallas kernels, shards(): pl.pallas_call(kernel, out_shape=(pltpu.VMEM((256, 256), F32), pltpu.VMEM...  40.8 us

profile of v10, /device:TPU:1, one launch (start us, length us, event | category | flops | bytes accessed | tf_op | source)
XLA Modules:
  0.0 42.6 jit_solution(7973097917055751048)
XLA Ops:
  0.6 40.8 %shard_map.50 = (f32[256,256]{1,0:T(8,128)S(1)}, f32[8,128]{1,0:T(8,128)S(1)}) custom-call(f32[256,256]{1,0:T(8,128)} %bitcast.5, f32[1168,256]{1,0:T(8,128)} %constant.4.clone.plain_hbm, bf16[1920,256]{1,0:T(8,128)(2,1)} %constant.5.clone.narrow_hbm), custom_call_target="tpu_custom_call" | custom-call | tf_op jit(solution)/shard_map/pallas_call | solution.py:656
  41.4 0.7 %copy.6 = f32[16,16,256]{2,1,0:T(8,128)} copy(f32[16,16,256]{2,1,0:T(8,128)S(1)} %bitcast.4) | data formatting | bytes 524288
  42.1 0.5 %slice_bitcast_fusion = f32[2]{0:T(128)} fusion(f32[8,128]{1,0:T(8,128)S(1)} %get-tuple-element.5), kind=kLoop, calls=%fused_computation | loop fusion | bytes 16 | tf_op jit(solution)/shard_map/squeeze | solution.py:697
